TPU v7x, 32 devices: a whole 2x2x4 slice. The times are simulated.
32 devices in a mesh: rep: 2 (over x), dp: 16 (over y, z, core).
Axes of the slice: x: 2, y: 2, z: 4, core: 2. Of those that a mesh axis runs over, the one named last changes fastest.
Arguments:
- x: bfloat16 [32, 2048, 896], P(('rep', 'dp')), parts along dimension 0
- dy: bfloat16 [32, 2048, 896], P(('rep', 'dp')), parts along dimension 0
- w_gate: bfloat16 [2, 896, 2560], P(None, 'dp')
- w_up: bfloat16 [2, 896, 2560], P(None, 'dp')
- w_down: bfloat16 [2, 2560, 896], P(None, 'dp')
Outputs:
- output 1: bfloat16 [32, 2048, 896], P(('rep', 'dp')), parts along dimension 0
- output 2: bfloat16 [4, 896, 2560], P('rep', 'dp'), parts along dimension 0
- output 3: bfloat16 [4, 896, 2560], P('rep', 'dp'), parts along dimension 0
- output 4: bfloat16 [4, 2560, 896], P('rep', 'dp'), parts along dimension 0
There are 2 independent parts. A program takes and returns all parts, laid end to end along the dimension named above; an argument that names none is the same for every part.
All inputs are finite; a program needn't handle non-finite values.
Results may differ from a plain program's by a relative error of at most 0.018.
Values are sent between devices in bfloat16 or wider.
A program may use at most 2 GiB of HBM per device.

v0:
```python
import jax
import jax.numpy as jnp
from jax import lax

NAMES = ("w_gate", "w_up", "w_down")


def matmul(a, w):
    return jnp.dot(a, w, preferred_element_type=jnp.float32).astype(jnp.bfloat16)


def normed(h):
    wide = h.astype(jnp.float32)
    scale = lax.rsqrt(jnp.mean(wide**2, -1, keepdims=True) + 1e-6)
    return (wide * scale).astype(jnp.bfloat16)


def layer(h, w):
    a = normed(h)
    gate = jnp.dot(a, w["w_gate"], preferred_element_type=jnp.float32)
    up = jnp.dot(a, w["w_up"], preferred_element_type=jnp.float32)
    return h + matmul((jax.nn.silu(gate) * up).astype(jnp.bfloat16), w["w_down"])


def stack(weights, h):
    for number in range(weights["w_gate"].shape[0]):
        h = layer(h, {name: w[number] for name, w in weights.items()})
    return h


def solution(mesh):
    groups = mesh.shape["rep"]

    def step(x, dy, *weights):
        shape = x.shape
        x, dy = (t.reshape(groups, -1, *t.shape[1:]) for t in (x, dy))

        def of_a_group(x, dy):
            _, back = jax.vjp(stack, dict(zip(NAMES, weights, strict=True)), x)
            by_weights, by_x = back(dy)
            return (by_x, *(by_weights[name] for name in NAMES))

        by_x, *by_weights = jax.vmap(of_a_group)(x, dy)
        return (by_x.reshape(shape), *(t.reshape(-1, *t.shape[2:]) for t in by_weights))

    return step
```

profile of v0, /device:TPU:0, one launch (start us, length us, event | category | flops | bytes accessed | tf_op | source)
XLA Modules:
  0.0 1359.2 jit_solution(15326568873116063597)
XLA Ops:
  17.7 6.1 copy.1
  23.9 6.2 copy
  30.1 6.1 copy.3
  36.8 28.4 %all-gather.30.cloned.1.call-done = bf16[1,896,2560]{2,1,0:T(8,128)(2,1)} async-done(((bf16[1,56,2560]{2,1,0:T(8,128)(2,1)}), bf16[1,896,2560]{2,1,0:T(8,128)(2,1)}) %all-gather.30.cloned.1.call-update) | async-done | bytes 4587536 | tf_op jit(solution)/vmap(jvp())/squeeze | solution.py:27
  65.2 18.1 %fusion.190 = f32[2048,2560]{1,0:T(8,128)} fusion(bf16[1,896,2560]{2,1,0:T(8,128)(2,1)} %all-gather.30.cloned.1.call-done, bf16[1,2048,896]{2,1,0:T(8,128)(2,1)} %param.13, f32[2048]{0:T(1024)S(1)} %get-tuple-element.267), kind=kOutput, calls=%fused_computation.241 | convolution fusion | flops 9400745984 | bytes 29237248 | tf_op jit(solution)/vmap(jvp())/dot_general | solution.py:20
  83.3 35.4 %all-gather.32.cloned.1.call-done = bf16[1,896,2560]{2,1,0:T(8,128)(2,1)} async-done(((bf16[1,56,2560]{2,1,0:T(8,128)(2,1)}), bf16[1,896,2560]{2,1,0:T(8,128)(2,1)}) %all-gather.32.cloned.1.call-update) | async-done | bytes 4587536 | tf_op jit(solution)/vmap(jvp())/squeeze | solution.py:27
  118.7 26.0 %fusion.160 = (bf16[1,1,2048,2560]{3,2,1,0:T(8,128)(2,1)}, f32[2048,2560]{1,0:T(8,128)}) fusion(f32[2048,2560]{1,0:T(8,128)} %fusion.190, bf16[1,896,2560]{2,1,0:T(8,128)(2,1)} %all-gather.32.cloned.1.call-done, bf16[1,2048,896]{2,1,0:T(8,128)(2,1)} %param.13, f32[2048]{0:T(1024)S(1)} %get-tuple-element.267), kind=kOutput, calls=%fused_computation.195 | convolution fusion | flops 9432203264 | bytes 60694528 | tf_op jit(solution)/vmap(jvp())/dot_general | solution.py:21
  144.7 27.5 %all-gather.34.cloned.1.call-done = bf16[1,2560,896]{2,1,0:T(8,128)(2,1)} async-done(((bf16[1,160,896]{2,1,0:T(8,128)(2,1)}), bf16[1,2560,896]{2,1,0:T(8,128)(2,1)}) %all-gather.34.cloned.1.call-update) | async-done | bytes 4587536 | tf_op jit(solution)/vmap(jvp())/squeeze | solution.py:27
  172.2 15.1 %fusion.174 = (f32[2048]{0:T(1024)S(1)}, bf16[1,1,2048,896]{2,3,1,0:T(8,128)(2,1)S(1)}) fusion(bf16[1,2560,896]{2,1,0:T(8,128)(2,1)} %all-gather.34.cloned.1.call-done, bf16[1,1,2048,2560]{3,2,1,0:T(8,128)(2,1)} %get-tuple-element.268, bf16[1,2048,896]{1,2,0:T(8,128)(2,1)} %copy.1), kind=kOutput, calls=%fused_computation.225 | convolution fusion | flops 9404413952 | bytes 22421504 | tf_op jit(solution)/vmap(jvp())/dot_general | solution.py:9
  192.1 33.6 %all-gather.36.cloned.1.call-done = bf16[1,896,2560]{2,1,0:T(8,128)(2,1)} async-done(((bf16[1,56,2560]{2,1,0:T(8,128)(2,1)}), bf16[1,896,2560]{2,1,0:T(8,128)(2,1)}) %all-gather.36.cloned.1.call-update) | async-done | bytes 4587536 | tf_op jit(solution)/vmap(jvp())/squeeze | solution.py:27
  225.6 18.1 %fusion.182 = f32[2048,2560]{1,0:T(8,128)} fusion(bf16[1,896,2560]{2,1,0:T(8,128)(2,1)} %all-gather.36.cloned.1.call-done, bf16[1,1,2048,896]{2,3,1,0:T(8,128)(2,1)} %fusion.175), kind=kOutput, calls=%fused_computation.233 | convolution fusion | flops 9395240960 | bytes 29229056 | tf_op jit(solution)/vmap(jvp())/dot_general | solution.py:20
  243.7 35.3 %all-gather.40.cloned.1.call-done = bf16[1,896,2560]{2,1,0:T(8,128)(2,1)} async-done(((bf16[1,56,2560]{2,1,0:T(8,128)(2,1)}), bf16[1,896,2560]{2,1,0:T(8,128)(2,1)}) %all-gather.40.cloned.1.call-update) | async-done | bytes 4587536 | tf_op jit(solution)/vmap(jvp())/squeeze | solution.py:27
  279.0 25.7 %fusion.154 = (bf16[1,1,2048,2560]{3,2,1,0:T(8,128)(2,1)}, f32[2048,2560]{1,0:T(8,128)}) fusion(f32[2048,2560]{1,0:T(8,128)} %fusion.182, bf16[1,896,2560]{2,1,0:T(8,128)(2,1)} %all-gather.40.cloned.1.call-done, bf16[1,1,2048,896]{2,3,1,0:T(8,128)(2,1)} %fusion.175), kind=kOutput, calls=%fused_computation.185 | convolution fusion | flops 9426698240 | bytes 60686336 | tf_op jit(solution)/vmap(jvp())/dot_general | solution.py:21
  304.7 14.5 %copy.4 = bf16[1,1,2048,2560]{2,3,1,0:T(8,128)(2,1)} copy(bf16[1,1,2048,2560]{3,2,1,0:T(8,128)(2,1)} %get-tuple-element.268) | data formatting | bytes 20971520
  319.3 14.6 %copy.2 = bf16[1,1,2048,2560]{2,3,1,0:T(8,128)(2,1)} copy(bf16[1,1,2048,2560]{3,2,1,0:T(8,128)(2,1)} %get-tuple-element.275) | data formatting | bytes 20971520
  333.9 140.1 %while.16 = (bf16[1,1,2048,2560]{2,3,1,0:T(8,128)(2,1)}, bf16[1,1,2048,896]{3,2,1,0:T(8,128)(2,1)}, f32[1,160,896]{2,1,0:T(8,128)S(1)}, f32[1,160,896]{2,1,0:T(8...) while((bf16[1,1,2048,2560]{2,3,1,0:T(8,128)(2,1)}, ...), condition=%wide.windowed_dot_general_cond_rs.4.clone, body=%wide.windowed_dot_general_body_rs.4.clone.sunk | while | flops 2354913280 | bytes 48956004 | solution.py:9
  344.4 7.4 collective-permute-done.16
  361.0 6.4 collective-permute-done.18
  394.0 6.6 collective-permute-done.18
  428.6 8.2 collective-permute-done.18
  464.8 8.2 collective-permute-done.18
  474.8 28.1 %convert_multiply_fusion.3 = (bf16[1,1,2048,2560]{3,2,1,0:T(8,128)(2,1)}, bf16[1,1,2048,2560]{3,2,1,0:T(8,128)(2,1)S(1)}) fusion(f32[2048,2560]{1,0:T(8,128)} %fusion.182, f32[2048,2560]{1,0:T(8,128)} %get-tuple-element.276, bf16[1,2560,896]{2,1,0:T(8,128)(2,1)} %all-gather.38.cloned.1.call-done, bf16[1,2048,896]{2,1,0:T(8,128)(2,1)} %param.12), kind=kOutput, calls=%fused_computation.173 | convolution fusion | flops 9479127040 | bytes 71172096 | tf_op jit(solution)/vmap(transpose(jvp()))/dot_general | solution.py:9
  502.8 14.8 %fusion.152 = bf16[2048,896]{0,1:T(8,128)(2,1)} fusion(bf16[1,1,2048,2560]{3,2,1,0:T(8,128)(2,1)S(1)} %get-tuple-element.551, bf16[1,896,2560]{2,1,0:T(8,128)(2,1)} %all-gather.36.cloned.1.call-done), kind=kOutput, calls=%fused_computation.182 | convolution fusion | flops 9395240960 | bytes 18743296 | tf_op jit(solution)/vmap(transpose(jvp()))/dot_general | solution.py:20
  517.7 13.4 fusion.176
  535.7 6.1 copy.5
  541.9 142.0 %while.17 = (bf16[1,1,2048,2560]{2,3,1,0:T(8,128)(2,1)}, bf16[1,1,2048,896]{3,2,1,0:T(8,128)(2,1)}, f32[1,160,896]{2,1,0:T(8,128)S(1)}, f32[1,160,896]{2,1,0:T(8...) while((bf16[1,1,2048,2560]{2,3,1,0:T(8,128)(2,1)}, ...), condition=%wide.windowed_dot_general_cond_rs.5.clone, body=%wide.windowed_dot_general_body_rs.5.clone.sunk | while | flops 2354913280 | bytes 48956004 | solution.py:9
  552.1 7.8 collective-permute-done.20
  569.1 7.9 collective-permute-done.22
  603.9 8.3 collective-permute-done.22
  624.5 6.2 collective-permute-done.20
  639.8 8.3 collective-permute-done.22
  674.3 8.5 collective-permute-done.22
  684.7 143.5 %while.14 = (bf16[1,1,2048,896]{2,3,1,0:T(8,128)(2,1)}, bf16[1,1,2048,2560]{3,2,1,0:T(8,128)(2,1)}, f32[1,56,2560]{2,1,0:T(8,128)S(1)}, f32[1,56,2560]{2,1,0:T(8...) while((bf16[1,1,2048,896]{2,3,1,0:T(8,128)(2,1)}, ...), condition=%wide.windowed_dot_general_cond_rs.2.clone, body=%wide.windowed_dot_general_body_rs.2.clone.sunk | while | flops 2351505408 | bytes 105579168 | solution.py:21
  697.9 10.1 collective-permute-done.8
  714.4 7.3 collective-permute-done.10
  730.9 6.0 fusion.292
  747.3 9.6 collective-permute-done.10
  766.1 6.0 fusion.292
  780.3 9.5 collective-permute-done.10
  817.0 10.2 collective-permute-done.10
  829.0 28.3 %convert_multiply_fusion.1 = (bf16[1,1,2048,2560]{3,2,1,0:T(8,128)(2,1)}, bf16[1,1,2048,2560]{3,2,1,0:T(8,128)(2,1)S(1)}) fusion(f32[2048,2560]{1,0:T(8,128)} %fusion.190, f32[2048,2560]{1,0:T(8,128)} %get-tuple-element.269, bf16[1,2560,896]{2,1,0:T(8,128)(2,1)} %all-gather.34.cloned.1.call-done, bf16[1,1,2048,896]{2,3,1,0:T(8,128)(2,1)} %fusion.194), kind=kOutput, calls=%fused_computation.171 | convolution fusion | flops 9479127040 | bytes 71172096 | tf_op jit(solution)/vmap(transpose(jvp()))/dot_general | solution.py:9
  857.3 13.5 fusion.148
  870.9 16.9 %fusion.173 = (bf16[1,1,2048,896]{2,3,1,0:T(8,128)(2,1)}, f32[2048]{0:T(1024)}, bf16[2048,896]{0,1:T(8,128)(2,1)}) fusion(bf16[1,2048,896]{1,2,0:T(8,128)(2,1)S(1)} %copy-done.24, f32[2048]{0:T(1024)S(1)} %bitcast.580, bf16[2048,896]{0,1:T(8,128)(2,1)S(1)} %fusion.148, bf16[1,896,2560]{2,1,0:T(8,128)(2,1)} %all-gather.32.cloned.1.call-done, ...), kind=kOutput, calls=%fused_computation.224 | convolution fusion | flops 9408083968 | bytes 29769728 | tf_op jit(solution)/vmap(transpose(jvp()))/dot_general | solution.py:21
  887.8 139.7 %while.15 = (bf16[1,1,2048,896]{2,3,1,0:T(8,128)(2,1)}, bf16[1,1,2048,2560]{3,2,1,0:T(8,128)(2,1)}, f32[1,56,2560]{2,1,0:T(8,128)S(1)}, f32[1,56,2560]{2,1,0:T(8...) while((bf16[1,1,2048,896]{2,3,1,0:T(8,128)(2,1)}, ...), condition=%wide.windowed_dot_general_cond_rs.3.clone, body=%wide.windowed_dot_general_body_rs.3.clone.sunk | while | flops 2351505408 | bytes 105579168 | solution.py:21
  912.5 9.4 collective-permute-done.14
  947.8 10.2 collective-permute-done.14
  983.4 10.6 collective-permute-done.14
  1001.3 6.0 fusion.300
  1018.3 9.1 collective-permute-done.14
  1028.3 143.5 %while.12 = (bf16[1,1,2048,896]{2,3,1,0:T(8,128)(2,1)}, bf16[1,1,2048,2560]{3,2,1,0:T(8,128)(2,1)}, f32[1,56,2560]{2,1,0:T(8,128)S(1)}, f32[1,56,2560]{2,1,0:T(8...) while((bf16[1,1,2048,896]{2,3,1,0:T(8,128)(2,1)}, ...), condition=%wide.windowed_dot_general_cond_rs.clone, body=%wide.windowed_dot_general_body_rs.clone.sunk | while | flops 2351505408 | bytes 105579168 | solution.py:20
  1053.0 10.2 collective-permute-done.2
  1089.2 10.5 collective-permute-done.2
  1124.5 10.2 collective-permute-done.2
  1160.4 10.3 collective-permute-done.2
  1172.7 143.3 %while.13 = (bf16[1,1,2048,896]{2,3,1,0:T(8,128)(2,1)}, bf16[1,1,2048,2560]{3,2,1,0:T(8,128)(2,1)}, f32[1,56,2560]{2,1,0:T(8,128)S(1)}, f32[1,56,2560]{2,1,0:T(8...) while((bf16[1,1,2048,896]{2,3,1,0:T(8,128)(2,1)}, ...), condition=%wide.windowed_dot_general_cond_rs.1.clone, body=%wide.windowed_dot_general_body_rs.1.clone.sunk | while | flops 2351505408 | bytes 105579168 | solution.py:20
  1197.3 10.3 collective-permute-done.6
  1216.5 6.0 fusion.284
  1233.0 10.3 collective-permute-done.6
  1269.1 10.4 collective-permute-done.6
  1288.4 6.0 fusion.284
  1304.8 10.3 collective-permute-done.6
  1317.4 9.0 fusion.193
  1326.5 6.2 copy.6
  1333.5 11.1 collective-permute-start.25
  (518 shorter events, 556.4 us)
Async XLA Ops:
  7.2 58.0 %all-gather.30.cloned.1.call-start = ((), (), s32[]{:S(2)}) async-start(), calls=%async_computation | async-start | bytes 4874240 | tf_op jit(solution)/vmap(jvp())/squeeze | solution.py:27
  9.2 109.5 %all-gather.32.cloned.1.call-start = ((), (), s32[]{:S(2)}) async-start(), calls=%async_computation.1 | async-start | bytes 4874240 | tf_op jit(solution)/vmap(jvp())/squeeze | solution.py:27
  11.2 161.1 %all-gather.34.cloned.1.call-start = ((), (), s32[]{:S(2)}) async-start(), calls=%async_computation.2 | async-start | bytes 4874240 | tf_op jit(solution)/vmap(jvp())/squeeze | solution.py:27
  13.2 212.4 %all-gather.36.cloned.1.call-start = ((), (), s32[]{:S(2)}) async-start(), calls=%async_computation.3 | async-start | bytes 4874240 | tf_op jit(solution)/vmap(jvp())/squeeze | solution.py:27
  13.8 265.2 %all-gather.40.cloned.1.call-start = ((), (), s32[]{:S(2)}) async-start(), calls=%async_computation.5 | async-start | bytes 4874240 | tf_op jit(solution)/vmap(jvp())/squeeze | solution.py:27
  14.3 459.6 %all-gather.38.cloned.1.call-start = ((), (), s32[]{:S(2)}) async-start(), calls=%async_computation.4 | async-start | bytes 4874240 | tf_op jit(solution)/vmap(jvp())/squeeze | solution.py:27
  333.9 17.9 %collective-permute-start.16 = (f32[1,160,896]{2,1,0:T(8,128)S(1)}, f32[1,160,896]{2,1,0:T(8,128)S(1)}, u32[]{:S(2)}, u32[]{:S(2)}) collective-permute-start(f32[1,160,896]{2,1,0:T(8,128)S(1)} %broadcast_select_fusion.32), channel_id=39, source_target_pairs={{0,1},{1,2},{2,3},{3,4},{4,5},{5,6},{6,7},{7,8},{8,9},{9,10},{10,1... | collective-permute-start | bytes 1720328 | tf_op jit(solution)/vmap(transpose(jvp()))/dot_general | solution.py:9
  334.3 17.5 %collective-permute-start.17 = (f32[1,160,896]{2,1,0:T(8,128)S(1)}, f32[1,160,896]{2,1,0:T(8,128)S(1)}, u32[]{:S(2)}, u32[]{:S(2)}) collective-permute-start(f32[1,160,896]{2,1,0:T(8,128)S(1)} %broadcast_select_fusion.33), channel_id=38, source_target_pairs={{0,15},{1,0},{2,1},{3,2},{4,3},{5,4},{6,5},{7,6},{8,7},{9,8},{10,9... | collective-permute-start | bytes 1720328 | tf_op jit(solution)/vmap(transpose(jvp()))/dot_general | solution.py:9
  402.8 16.4 %collective-permute-start.17 = (f32[1,160,896]{2,1,0:T(8,128)S(1)}, f32[1,160,896]{2,1,0:T(8,128)S(1)}, u32[]{:S(2)}, u32[]{:S(2)}) collective-permute-start(f32[1,160,896]{2,1,0:T(8,128)S(1)} %broadcast_select_fusion.33), channel_id=38, source_target_pairs={{0,15},{1,0},{2,1},{3,2},{4,3},{5,4},{6,5},{7,6},{8,7},{9,8},{10,9... | collective-permute-start | bytes 1720328 | tf_op jit(solution)/vmap(transpose(jvp()))/dot_general | solution.py:9
  419.3 17.5 %collective-permute-start.18 = (f32[1,160,896]{2,1,0:T(8,128)S(1)}, f32[1,160,896]{2,1,0:T(8,128)S(1)}, u32[]{:S(2)}, u32[]{:S(2)}) collective-permute-start(f32[1,160,896]{2,1,0:T(8,128)S(1)} %get-tuple-element.498), channel_id=41, source_target_pairs={{0,1},{1,2},{2,3},{3,4},{4,5},{5,6},{6,7},{7,8},{8,9},{9,10},{10,1... | collective-permute-start | bytes 1720328 | tf_op jit(solution)/vmap(transpose(jvp()))/dot_general | solution.py:9
  419.3 17.5 %collective-permute-start.19 = (f32[1,160,896]{2,1,0:T(8,128)S(1)}, f32[1,160,896]{2,1,0:T(8,128)S(1)}, u32[]{:S(2)}, u32[]{:S(2)}) collective-permute-start(f32[1,160,896]{2,1,0:T(8,128)S(1)} %get-tuple-element.499), channel_id=40, source_target_pairs={{0,15},{1,0},{2,1},{3,2},{4,3},{5,4},{6,5},{7,6},{8,7},{9,8},{10,9... | collective-permute-start | bytes 1720328 | tf_op jit(solution)/vmap(transpose(jvp()))/dot_general | solution.py:9
  438.8 16.4 %collective-permute-start.16 = (f32[1,160,896]{2,1,0:T(8,128)S(1)}, f32[1,160,896]{2,1,0:T(8,128)S(1)}, u32[]{:S(2)}, u32[]{:S(2)}) collective-permute-start(f32[1,160,896]{2,1,0:T(8,128)S(1)} %broadcast_select_fusion.32), channel_id=39, source_target_pairs={{0,1},{1,2},{2,3},{3,4},{4,5},{5,6},{6,7},{7,8},{8,9},{9,10},{10,1... | collective-permute-start | bytes 1720328 | tf_op jit(solution)/vmap(transpose(jvp()))/dot_general | solution.py:9
  439.0 16.4 %collective-permute-start.17 = (f32[1,160,896]{2,1,0:T(8,128)S(1)}, f32[1,160,896]{2,1,0:T(8,128)S(1)}, u32[]{:S(2)}, u32[]{:S(2)}) collective-permute-start(f32[1,160,896]{2,1,0:T(8,128)S(1)} %broadcast_select_fusion.33), channel_id=38, source_target_pairs={{0,15},{1,0},{2,1},{3,2},{4,3},{5,4},{6,5},{7,6},{8,7},{9,8},{10,9... | collective-permute-start | bytes 1720328 | tf_op jit(solution)/vmap(transpose(jvp()))/dot_general | solution.py:9
  455.5 17.5 %collective-permute-start.18 = (f32[1,160,896]{2,1,0:T(8,128)S(1)}, f32[1,160,896]{2,1,0:T(8,128)S(1)}, u32[]{:S(2)}, u32[]{:S(2)}) collective-permute-start(f32[1,160,896]{2,1,0:T(8,128)S(1)} %get-tuple-element.498), channel_id=41, source_target_pairs={{0,1},{1,2},{2,3},{3,4},{4,5},{5,6},{6,7},{7,8},{8,9},{9,10},{10,1... | collective-permute-start | bytes 1720328 | tf_op jit(solution)/vmap(transpose(jvp()))/dot_general | solution.py:9
  455.5 17.5 %collective-permute-start.19 = (f32[1,160,896]{2,1,0:T(8,128)S(1)}, f32[1,160,896]{2,1,0:T(8,128)S(1)}, u32[]{:S(2)}, u32[]{:S(2)}) collective-permute-start(f32[1,160,896]{2,1,0:T(8,128)S(1)} %get-tuple-element.499), channel_id=40, source_target_pairs={{0,15},{1,0},{2,1},{3,2},{4,3},{5,4},{6,5},{7,6},{8,7},{9,8},{10,9... | collective-permute-start | bytes 1720328 | tf_op jit(solution)/vmap(transpose(jvp()))/dot_general | solution.py:9
  473.9 859.5 %collective-permute-start.28 = (f32[1,160,896]{2,1,0:T(8,128)}, f32[1,160,896]{2,1,0:T(8,128)}, u32[]{:S(2)}, u32[]{:S(2)}) collective-permute-start(f32[1,160,896]{2,1,0:T(8,128)} %get-tuple-element.45), channel_id=42, source_target_pairs={{0,1},{1,2},{2,3},{3,4},{4,5},{5,6},{6,7},{7,8},{8,9},{9,10},{10,1... | collective-permute-start | bytes 1720328 | tf_op jit(solution)/vmap(transpose(jvp()))/dot_general | solution.py:9
  541.9 18.0 %collective-permute-start.20 = (f32[1,160,896]{2,1,0:T(8,128)S(1)}, f32[1,160,896]{2,1,0:T(8,128)S(1)}, u32[]{:S(2)}, u32[]{:S(2)}) collective-permute-start(f32[1,160,896]{2,1,0:T(8,128)S(1)} %broadcast_select_fusion.34), channel_id=45, source_target_pairs={{0,1},{1,2},{2,3},{3,4},{4,5},{5,6},{6,7},{7,8},{8,9},{9,10},{10,1... | collective-permute-start | bytes 1720328 | tf_op jit(solution)/vmap(transpose(jvp()))/dot_general | solution.py:9
  542.0 17.9 %collective-permute-start.21 = (f32[1,160,896]{2,1,0:T(8,128)S(1)}, f32[1,160,896]{2,1,0:T(8,128)S(1)}, u32[]{:S(2)}, u32[]{:S(2)}) collective-permute-start(f32[1,160,896]{2,1,0:T(8,128)S(1)} %broadcast_select_fusion.35), channel_id=44, source_target_pairs={{0,15},{1,0},{2,1},{3,2},{4,3},{5,4},{6,5},{7,6},{8,7},{9,8},{10,9... | collective-permute-start | bytes 1720328 | tf_op jit(solution)/vmap(transpose(jvp()))/dot_general | solution.py:9
  560.1 17.0 %collective-permute-start.22 = (f32[1,160,896]{2,1,0:T(8,128)S(1)}, f32[1,160,896]{2,1,0:T(8,128)S(1)}, u32[]{:S(2)}, u32[]{:S(2)}) collective-permute-start(f32[1,160,896]{2,1,0:T(8,128)S(1)} %get-tuple-element.507), channel_id=47, source_target_pairs={{0,1},{1,2},{2,3},{3,4},{4,5},{5,6},{6,7},{7,8},{8,9},{9,10},{10,1... | collective-permute-start | bytes 1720328 | tf_op jit(solution)/vmap(transpose(jvp()))/dot_general | solution.py:9
  560.2 16.9 %collective-permute-start.23 = (f32[1,160,896]{2,1,0:T(8,128)S(1)}, f32[1,160,896]{2,1,0:T(8,128)S(1)}, u32[]{:S(2)}, u32[]{:S(2)}) collective-permute-start(f32[1,160,896]{2,1,0:T(8,128)S(1)} %get-tuple-element.508), channel_id=46, source_target_pairs={{0,15},{1,0},{2,1},{3,2},{4,3},{5,4},{6,5},{7,6},{8,7},{9,8},{10,9... | collective-permute-start | bytes 1720328 | tf_op jit(solution)/vmap(transpose(jvp()))/dot_general | solution.py:9
  594.7 17.5 %collective-permute-start.22 = (f32[1,160,896]{2,1,0:T(8,128)S(1)}, f32[1,160,896]{2,1,0:T(8,128)S(1)}, u32[]{:S(2)}, u32[]{:S(2)}) collective-permute-start(f32[1,160,896]{2,1,0:T(8,128)S(1)} %get-tuple-element.507), channel_id=47, source_target_pairs={{0,1},{1,2},{2,3},{3,4},{4,5},{5,6},{6,7},{7,8},{8,9},{9,10},{10,1... | collective-permute-start | bytes 1720328 | tf_op jit(solution)/vmap(transpose(jvp()))/dot_general | solution.py:9
  594.7 17.5 %collective-permute-start.23 = (f32[1,160,896]{2,1,0:T(8,128)S(1)}, f32[1,160,896]{2,1,0:T(8,128)S(1)}, u32[]{:S(2)}, u32[]{:S(2)}) collective-permute-start(f32[1,160,896]{2,1,0:T(8,128)S(1)} %get-tuple-element.508), channel_id=46, source_target_pairs={{0,15},{1,0},{2,1},{3,2},{4,3},{5,4},{6,5},{7,6},{8,7},{9,8},{10,9... | collective-permute-start | bytes 1720328 | tf_op jit(solution)/vmap(transpose(jvp()))/dot_general | solution.py:9
  614.2 16.4 %collective-permute-start.20 = (f32[1,160,896]{2,1,0:T(8,128)S(1)}, f32[1,160,896]{2,1,0:T(8,128)S(1)}, u32[]{:S(2)}, u32[]{:S(2)}) collective-permute-start(f32[1,160,896]{2,1,0:T(8,128)S(1)} %broadcast_select_fusion.34), channel_id=45, source_target_pairs={{0,1},{1,2},{2,3},{3,4},{4,5},{5,6},{6,7},{7,8},{8,9},{9,10},{10,1... | collective-permute-start | bytes 1720328 | tf_op jit(solution)/vmap(transpose(jvp()))/dot_general | solution.py:9
  614.4 16.3 %collective-permute-start.21 = (f32[1,160,896]{2,1,0:T(8,128)S(1)}, f32[1,160,896]{2,1,0:T(8,128)S(1)}, u32[]{:S(2)}, u32[]{:S(2)}) collective-permute-start(f32[1,160,896]{2,1,0:T(8,128)S(1)} %broadcast_select_fusion.35), channel_id=44, source_target_pairs={{0,15},{1,0},{2,1},{3,2},{4,3},{5,4},{6,5},{7,6},{8,7},{9,8},{10,9... | collective-permute-start | bytes 1720328 | tf_op jit(solution)/vmap(transpose(jvp()))/dot_general | solution.py:9
  630.8 17.3 %collective-permute-start.22 = (f32[1,160,896]{2,1,0:T(8,128)S(1)}, f32[1,160,896]{2,1,0:T(8,128)S(1)}, u32[]{:S(2)}, u32[]{:S(2)}) collective-permute-start(f32[1,160,896]{2,1,0:T(8,128)S(1)} %get-tuple-element.507), channel_id=47, source_target_pairs={{0,1},{1,2},{2,3},{3,4},{4,5},{5,6},{6,7},{7,8},{8,9},{9,10},{10,1... | collective-permute-start | bytes 1720328 | tf_op jit(solution)/vmap(transpose(jvp()))/dot_general | solution.py:9
  630.9 17.2 %collective-permute-start.23 = (f32[1,160,896]{2,1,0:T(8,128)S(1)}, f32[1,160,896]{2,1,0:T(8,128)S(1)}, u32[]{:S(2)}, u32[]{:S(2)}) collective-permute-start(f32[1,160,896]{2,1,0:T(8,128)S(1)} %get-tuple-element.508), channel_id=46, source_target_pairs={{0,15},{1,0},{2,1},{3,2},{4,3},{5,4},{6,5},{7,6},{8,7},{9,8},{10,9... | collective-permute-start | bytes 1720328 | tf_op jit(solution)/vmap(transpose(jvp()))/dot_general | solution.py:9
  665.3 17.6 %collective-permute-start.22 = (f32[1,160,896]{2,1,0:T(8,128)S(1)}, f32[1,160,896]{2,1,0:T(8,128)S(1)}, u32[]{:S(2)}, u32[]{:S(2)}) collective-permute-start(f32[1,160,896]{2,1,0:T(8,128)S(1)} %get-tuple-element.507), channel_id=47, source_target_pairs={{0,1},{1,2},{2,3},{3,4},{4,5},{5,6},{6,7},{7,8},{8,9},{9,10},{10,1... | collective-permute-start | bytes 1720328 | tf_op jit(solution)/vmap(transpose(jvp()))/dot_general | solution.py:9
  665.4 17.5 %collective-permute-start.23 = (f32[1,160,896]{2,1,0:T(8,128)S(1)}, f32[1,160,896]{2,1,0:T(8,128)S(1)}, u32[]{:S(2)}, u32[]{:S(2)}) collective-permute-start(f32[1,160,896]{2,1,0:T(8,128)S(1)} %get-tuple-element.508), channel_id=46, source_target_pairs={{0,15},{1,0},{2,1},{3,2},{4,3},{5,4},{6,5},{7,6},{8,7},{9,8},{10,9... | collective-permute-start | bytes 1720328 | tf_op jit(solution)/vmap(transpose(jvp()))/dot_general | solution.py:9
  683.9 664.1 %collective-permute-start.29 = (f32[1,160,896]{2,1,0:T(8,128)}, f32[1,160,896]{2,1,0:T(8,128)}, u32[]{:S(2)}, u32[]{:S(2)}) collective-permute-start(f32[1,160,896]{2,1,0:T(8,128)} %get-tuple-element.47), channel_id=48, source_target_pairs={{0,1},{1,2},{2,3},{3,4},{4,5},{5,6},{6,7},{7,8},{8,9},{9,10},{10,1... | collective-permute-start | bytes 1720328 | tf_op jit(solution)/vmap(transpose(jvp()))/dot_general | solution.py:9
  684.7 23.3 %collective-permute-start.8 = (f32[1,56,2560]{2,1,0:T(8,128)S(1)}, f32[1,56,2560]{2,1,0:T(8,128)S(1)}, u32[]{:S(2)}, u32[]{:S(2)}) collective-permute-start(f32[1,56,2560]{2,1,0:T(8,128)S(1)} %broadcast_select_fusion.28), channel_id=27, source_target_pairs={{0,1},{1,2},{2,3},{3,4},{4,5},{5,6},{6,7},{7,8},{8,9},{9,10},{10,1... | collective-permute-start | bytes 1720328 | tf_op jit(solution)/vmap(transpose(jvp()))/dot_general | solution.py:21
  684.8 23.2 %collective-permute-start.9 = (f32[1,56,2560]{2,1,0:T(8,128)S(1)}, f32[1,56,2560]{2,1,0:T(8,128)S(1)}, u32[]{:S(2)}, u32[]{:S(2)}) collective-permute-start(f32[1,56,2560]{2,1,0:T(8,128)S(1)} %broadcast_select_fusion.29), channel_id=26, source_target_pairs={{0,15},{1,0},{2,1},{3,2},{4,3},{5,4},{6,5},{7,6},{8,7},{9,8},{10,9... | collective-permute-start | bytes 1720328 | tf_op jit(solution)/vmap(transpose(jvp()))/dot_general | solution.py:21
  723.7 17.2 %collective-permute-start.8 = (f32[1,56,2560]{2,1,0:T(8,128)S(1)}, f32[1,56,2560]{2,1,0:T(8,128)S(1)}, u32[]{:S(2)}, u32[]{:S(2)}) collective-permute-start(f32[1,56,2560]{2,1,0:T(8,128)S(1)} %broadcast_select_fusion.28), channel_id=27, source_target_pairs={{0,1},{1,2},{2,3},{3,4},{4,5},{5,6},{6,7},{7,8},{8,9},{9,10},{10,1... | collective-permute-start | bytes 1720328 | tf_op jit(solution)/vmap(transpose(jvp()))/dot_general | solution.py:21
  793.1 17.4 %collective-permute-start.8 = (f32[1,56,2560]{2,1,0:T(8,128)S(1)}, f32[1,56,2560]{2,1,0:T(8,128)S(1)}, u32[]{:S(2)}, u32[]{:S(2)}) collective-permute-start(f32[1,56,2560]{2,1,0:T(8,128)S(1)} %broadcast_select_fusion.28), channel_id=27, source_target_pairs={{0,1},{1,2},{2,3},{3,4},{4,5},{5,6},{6,7},{7,8},{8,9},{9,10},{10,1... | collective-permute-start | bytes 1720328 | tf_op jit(solution)/vmap(transpose(jvp()))/dot_general | solution.py:21
  810.7 16.5 %collective-permute-start.10 = (f32[1,56,2560]{2,1,0:T(8,128)S(1)}, f32[1,56,2560]{2,1,0:T(8,128)S(1)}, u32[]{:S(2)}, u32[]{:S(2)}) collective-permute-start(f32[1,56,2560]{2,1,0:T(8,128)S(1)} %get-tuple-element.480), channel_id=29, source_target_pairs={{0,1},{1,2},{2,3},{3,4},{4,5},{5,6},{6,7},{7,8},{8,9},{9,10},{10,1... | collective-permute-start | bytes 1720328 | tf_op jit(solution)/vmap(transpose(jvp()))/dot_general | solution.py:21
  828.2 517.6 %collective-permute-start.26 = (f32[1,56,2560]{2,1,0:T(8,128)}, f32[1,56,2560]{2,1,0:T(8,128)}, u32[]{:S(2)}, u32[]{:S(2)}) collective-permute-start(f32[1,56,2560]{2,1,0:T(8,128)} %get-tuple-element.41), channel_id=30, source_target_pairs={{0,1},{1,2},{2,3},{3,4},{4,5},{5,6},{6,7},{7,8},{8,9},{9,10},{10,1... | collective-permute-start | bytes 1720328 | tf_op jit(solution)/vmap(transpose(jvp()))/dot_general | solution.py:21
  888.1 18.0 %collective-permute-start.12 = (f32[1,56,2560]{2,1,0:T(8,128)S(1)}, f32[1,56,2560]{2,1,0:T(8,128)S(1)}, u32[]{:S(2)}, u32[]{:S(2)}) collective-permute-start(f32[1,56,2560]{2,1,0:T(8,128)S(1)} %broadcast_select_fusion.30), channel_id=33, source_target_pairs={{0,1},{1,2},{2,3},{3,4},{4,5},{5,6},{6,7},{7,8},{8,9},{9,10},{10,1... | collective-permute-start | bytes 1720328 | tf_op jit(solution)/vmap(transpose(jvp()))/dot_general | solution.py:21
  888.6 17.5 %collective-permute-start.13 = (f32[1,56,2560]{2,1,0:T(8,128)S(1)}, f32[1,56,2560]{2,1,0:T(8,128)S(1)}, u32[]{:S(2)}, u32[]{:S(2)}) collective-permute-start(f32[1,56,2560]{2,1,0:T(8,128)S(1)} %broadcast_select_fusion.31), channel_id=32, source_target_pairs={{0,15},{1,0},{2,1},{3,2},{4,3},{5,4},{6,5},{7,6},{8,7},{9,8},{10,9... | collective-permute-start | bytes 1720328 | tf_op jit(solution)/vmap(transpose(jvp()))/dot_general | solution.py:21
  923.9 17.4 %collective-permute-start.12 = (f32[1,56,2560]{2,1,0:T(8,128)S(1)}, f32[1,56,2560]{2,1,0:T(8,128)S(1)}, u32[]{:S(2)}, u32[]{:S(2)}) collective-permute-start(f32[1,56,2560]{2,1,0:T(8,128)S(1)} %broadcast_select_fusion.30), channel_id=33, source_target_pairs={{0,1},{1,2},{2,3},{3,4},{4,5},{5,6},{6,7},{7,8},{8,9},{9,10},{10,1... | collective-permute-start | bytes 1720328 | tf_op jit(solution)/vmap(transpose(jvp()))/dot_general | solution.py:21
  941.5 16.5 %collective-permute-start.14 = (f32[1,56,2560]{2,1,0:T(8,128)S(1)}, f32[1,56,2560]{2,1,0:T(8,128)S(1)}, u32[]{:S(2)}, u32[]{:S(2)}) collective-permute-start(f32[1,56,2560]{2,1,0:T(8,128)S(1)} %get-tuple-element.489), channel_id=35, source_target_pairs={{0,1},{1,2},{2,3},{3,4},{4,5},{5,6},{6,7},{7,8},{8,9},{9,10},{10,1... | collective-permute-start | bytes 1720328 | tf_op jit(solution)/vmap(transpose(jvp()))/dot_general | solution.py:21
  959.5 17.4 %collective-permute-start.12 = (f32[1,56,2560]{2,1,0:T(8,128)S(1)}, f32[1,56,2560]{2,1,0:T(8,128)S(1)}, u32[]{:S(2)}, u32[]{:S(2)}) collective-permute-start(f32[1,56,2560]{2,1,0:T(8,128)S(1)} %broadcast_select_fusion.30), channel_id=33, source_target_pairs={{0,1},{1,2},{2,3},{3,4},{4,5},{5,6},{6,7},{7,8},{8,9},{9,10},{10,1... | collective-permute-start | bytes 1720328 | tf_op jit(solution)/vmap(transpose(jvp()))/dot_general | solution.py:21
  977.1 16.8 %collective-permute-start.14 = (f32[1,56,2560]{2,1,0:T(8,128)S(1)}, f32[1,56,2560]{2,1,0:T(8,128)S(1)}, u32[]{:S(2)}, u32[]{:S(2)}) collective-permute-start(f32[1,56,2560]{2,1,0:T(8,128)S(1)} %get-tuple-element.489), channel_id=35, source_target_pairs={{0,1},{1,2},{2,3},{3,4},{4,5},{5,6},{6,7},{7,8},{8,9},{9,10},{10,1... | collective-permute-start | bytes 1720328 | tf_op jit(solution)/vmap(transpose(jvp()))/dot_general | solution.py:21
  994.2 17.7 %collective-permute-start.12 = (f32[1,56,2560]{2,1,0:T(8,128)S(1)}, f32[1,56,2560]{2,1,0:T(8,128)S(1)}, u32[]{:S(2)}, u32[]{:S(2)}) collective-permute-start(f32[1,56,2560]{2,1,0:T(8,128)S(1)} %broadcast_select_fusion.30), channel_id=33, source_target_pairs={{0,1},{1,2},{2,3},{3,4},{4,5},{5,6},{6,7},{7,8},{8,9},{9,10},{10,1... | collective-permute-start | bytes 1720328 | tf_op jit(solution)/vmap(transpose(jvp()))/dot_general | solution.py:21
  994.3 17.5 %collective-permute-start.13 = (f32[1,56,2560]{2,1,0:T(8,128)S(1)}, f32[1,56,2560]{2,1,0:T(8,128)S(1)}, u32[]{:S(2)}, u32[]{:S(2)}) collective-permute-start(f32[1,56,2560]{2,1,0:T(8,128)S(1)} %broadcast_select_fusion.31), channel_id=32, source_target_pairs={{0,15},{1,0},{2,1},{3,2},{4,3},{5,4},{6,5},{7,6},{8,7},{9,8},{10,9... | collective-permute-start | bytes 1720328 | tf_op jit(solution)/vmap(transpose(jvp()))/dot_general | solution.py:21
  1029.2 17.4 %collective-permute-start = (f32[1,56,2560]{2,1,0:T(8,128)}, f32[1,56,2560]{2,1,0:T(8,128)S(1)}, u32[]{:S(2)}, u32[]{:S(2)}) collective-permute-start(f32[1,56,2560]{2,1,0:T(8,128)} %broadcast_select_fusion.24), channel_id=15, source_target_pairs={{0,1},{1,2},{2,3},{3,4},{4,5},{5,6},{6,7},{7,8},{8,9},{9,10},{10,1... | collective-permute-start | bytes 1720328 | tf_op jit(solution)/vmap(transpose(jvp()))/dot_general | solution.py:20
  1046.7 16.5 %collective-permute-start.2 = (f32[1,56,2560]{2,1,0:T(8,128)S(1)}, f32[1,56,2560]{2,1,0:T(8,128)S(1)}, u32[]{:S(2)}, u32[]{:S(2)}) collective-permute-start(f32[1,56,2560]{2,1,0:T(8,128)S(1)} %get-tuple-element.462), channel_id=17, source_target_pairs={{0,1},{1,2},{2,3},{3,4},{4,5},{5,6},{6,7},{7,8},{8,9},{9,10},{10,1... | collective-permute-start | bytes 1720328 | tf_op jit(solution)/vmap(transpose(jvp()))/dot_general | solution.py:20
  1065.5 17.4 %collective-permute-start = (f32[1,56,2560]{2,1,0:T(8,128)}, f32[1,56,2560]{2,1,0:T(8,128)S(1)}, u32[]{:S(2)}, u32[]{:S(2)}) collective-permute-start(f32[1,56,2560]{2,1,0:T(8,128)} %broadcast_select_fusion.24), channel_id=15, source_target_pairs={{0,1},{1,2},{2,3},{3,4},{4,5},{5,6},{6,7},{7,8},{8,9},{9,10},{10,1... | collective-permute-start | bytes 1720328 | tf_op jit(solution)/vmap(transpose(jvp()))/dot_general | solution.py:20
  1066.5 16.3 %collective-permute-start.1 = (f32[1,56,2560]{2,1,0:T(8,128)S(1)}, f32[1,56,2560]{2,1,0:T(8,128)S(1)}, u32[]{:S(2)}, u32[]{:S(2)}) collective-permute-start(f32[1,56,2560]{2,1,0:T(8,128)S(1)} %broadcast_select_fusion.25), channel_id=14, source_target_pairs={{0,15},{1,0},{2,1},{3,2},{4,3},{5,4},{6,5},{7,6},{8,7},{9,8},{10,9... | collective-permute-start | bytes 1720328 | tf_op jit(solution)/vmap(transpose(jvp()))/dot_general | solution.py:20
  1083.0 16.7 %collective-permute-start.2 = (f32[1,56,2560]{2,1,0:T(8,128)S(1)}, f32[1,56,2560]{2,1,0:T(8,128)S(1)}, u32[]{:S(2)}, u32[]{:S(2)}) collective-permute-start(f32[1,56,2560]{2,1,0:T(8,128)S(1)} %get-tuple-element.462), channel_id=17, source_target_pairs={{0,1},{1,2},{2,3},{3,4},{4,5},{5,6},{6,7},{7,8},{8,9},{9,10},{10,1... | collective-permute-start | bytes 1720328 | tf_op jit(solution)/vmap(transpose(jvp()))/dot_general | solution.py:20
  1100.8 17.4 %collective-permute-start = (f32[1,56,2560]{2,1,0:T(8,128)}, f32[1,56,2560]{2,1,0:T(8,128)S(1)}, u32[]{:S(2)}, u32[]{:S(2)}) collective-permute-start(f32[1,56,2560]{2,1,0:T(8,128)} %broadcast_select_fusion.24), channel_id=15, source_target_pairs={{0,1},{1,2},{2,3},{3,4},{4,5},{5,6},{6,7},{7,8},{8,9},{9,10},{10,1... | collective-permute-start | bytes 1720328 | tf_op jit(solution)/vmap(transpose(jvp()))/dot_general | solution.py:20
  1118.3 16.5 %collective-permute-start.2 = (f32[1,56,2560]{2,1,0:T(8,128)S(1)}, f32[1,56,2560]{2,1,0:T(8,128)S(1)}, u32[]{:S(2)}, u32[]{:S(2)}) collective-permute-start(f32[1,56,2560]{2,1,0:T(8,128)S(1)} %get-tuple-element.462), channel_id=17, source_target_pairs={{0,1},{1,2},{2,3},{3,4},{4,5},{5,6},{6,7},{7,8},{8,9},{9,10},{10,1... | collective-permute-start | bytes 1720328 | tf_op jit(solution)/vmap(transpose(jvp()))/dot_general | solution.py:20
  1136.6 17.4 %collective-permute-start = (f32[1,56,2560]{2,1,0:T(8,128)}, f32[1,56,2560]{2,1,0:T(8,128)S(1)}, u32[]{:S(2)}, u32[]{:S(2)}) collective-permute-start(f32[1,56,2560]{2,1,0:T(8,128)} %broadcast_select_fusion.24), channel_id=15, source_target_pairs={{0,1},{1,2},{2,3},{3,4},{4,5},{5,6},{6,7},{7,8},{8,9},{9,10},{10,1... | collective-permute-start | bytes 1720328 | tf_op jit(solution)/vmap(transpose(jvp()))/dot_general | solution.py:20
  1154.2 16.5 %collective-permute-start.2 = (f32[1,56,2560]{2,1,0:T(8,128)S(1)}, f32[1,56,2560]{2,1,0:T(8,128)S(1)}, u32[]{:S(2)}, u32[]{:S(2)}) collective-permute-start(f32[1,56,2560]{2,1,0:T(8,128)S(1)} %get-tuple-element.462), channel_id=17, source_target_pairs={{0,1},{1,2},{2,3},{3,4},{4,5},{5,6},{6,7},{7,8},{8,9},{9,10},{10,1... | collective-permute-start | bytes 1720328 | tf_op jit(solution)/vmap(transpose(jvp()))/dot_general | solution.py:20
  1173.5 17.4 %collective-permute-start.4 = (f32[1,56,2560]{2,1,0:T(8,128)}, f32[1,56,2560]{2,1,0:T(8,128)S(1)}, u32[]{:S(2)}, u32[]{:S(2)}) collective-permute-start(f32[1,56,2560]{2,1,0:T(8,128)} %broadcast_select_fusion.26), channel_id=21, source_target_pairs={{0,1},{1,2},{2,3},{3,4},{4,5},{5,6},{6,7},{7,8},{8,9},{9,10},{10,1... | collective-permute-start | bytes 1720328 | tf_op jit(solution)/vmap(transpose(jvp()))/dot_general | solution.py:20
  1191.0 16.5 %collective-permute-start.6 = (f32[1,56,2560]{2,1,0:T(8,128)S(1)}, f32[1,56,2560]{2,1,0:T(8,128)S(1)}, u32[]{:S(2)}, u32[]{:S(2)}) collective-permute-start(f32[1,56,2560]{2,1,0:T(8,128)S(1)} %get-tuple-element.471), channel_id=23, source_target_pairs={{0,1},{1,2},{2,3},{3,4},{4,5},{5,6},{6,7},{7,8},{8,9},{9,10},{10,1... | collective-permute-start | bytes 1720328 | tf_op jit(solution)/vmap(transpose(jvp()))/dot_general | solution.py:20
  1209.2 17.4 %collective-permute-start.4 = (f32[1,56,2560]{2,1,0:T(8,128)}, f32[1,56,2560]{2,1,0:T(8,128)S(1)}, u32[]{:S(2)}, u32[]{:S(2)}) collective-permute-start(f32[1,56,2560]{2,1,0:T(8,128)} %broadcast_select_fusion.26), channel_id=21, source_target_pairs={{0,1},{1,2},{2,3},{3,4},{4,5},{5,6},{6,7},{7,8},{8,9},{9,10},{10,1... | collective-permute-start | bytes 1720328 | tf_op jit(solution)/vmap(transpose(jvp()))/dot_general | solution.py:20
  1226.7 16.5 %collective-permute-start.6 = (f32[1,56,2560]{2,1,0:T(8,128)S(1)}, f32[1,56,2560]{2,1,0:T(8,128)S(1)}, u32[]{:S(2)}, u32[]{:S(2)}) collective-permute-start(f32[1,56,2560]{2,1,0:T(8,128)S(1)} %get-tuple-element.471), channel_id=23, source_target_pairs={{0,1},{1,2},{2,3},{3,4},{4,5},{5,6},{6,7},{7,8},{8,9},{9,10},{10,1... | collective-permute-start | bytes 1720328 | tf_op jit(solution)/vmap(transpose(jvp()))/dot_general | solution.py:20
  1245.4 17.4 %collective-permute-start.4 = (f32[1,56,2560]{2,1,0:T(8,128)}, f32[1,56,2560]{2,1,0:T(8,128)S(1)}, u32[]{:S(2)}, u32[]{:S(2)}) collective-permute-start(f32[1,56,2560]{2,1,0:T(8,128)} %broadcast_select_fusion.26), channel_id=21, source_target_pairs={{0,1},{1,2},{2,3},{3,4},{4,5},{5,6},{6,7},{7,8},{8,9},{9,10},{10,1... | collective-permute-start | bytes 1720328 | tf_op jit(solution)/vmap(transpose(jvp()))/dot_general | solution.py:20
  1262.9 16.6 %collective-permute-start.6 = (f32[1,56,2560]{2,1,0:T(8,128)S(1)}, f32[1,56,2560]{2,1,0:T(8,128)S(1)}, u32[]{:S(2)}, u32[]{:S(2)}) collective-permute-start(f32[1,56,2560]{2,1,0:T(8,128)S(1)} %get-tuple-element.471), channel_id=23, source_target_pairs={{0,1},{1,2},{2,3},{3,4},{4,5},{5,6},{6,7},{7,8},{8,9},{9,10},{10,1... | collective-permute-start | bytes 1720328 | tf_op jit(solution)/vmap(transpose(jvp()))/dot_general | solution.py:20
  1281.1 17.4 %collective-permute-start.4 = (f32[1,56,2560]{2,1,0:T(8,128)}, f32[1,56,2560]{2,1,0:T(8,128)S(1)}, u32[]{:S(2)}, u32[]{:S(2)}) collective-permute-start(f32[1,56,2560]{2,1,0:T(8,128)} %broadcast_select_fusion.26), channel_id=21, source_target_pairs={{0,1},{1,2},{2,3},{3,4},{4,5},{5,6},{6,7},{7,8},{8,9},{9,10},{10,1... | collective-permute-start | bytes 1720328 | tf_op jit(solution)/vmap(transpose(jvp()))/dot_general | solution.py:20
  1282.1 16.3 %collective-permute-start.5 = (f32[1,56,2560]{2,1,0:T(8,128)S(1)}, f32[1,56,2560]{2,1,0:T(8,128)S(1)}, u32[]{:S(2)}, u32[]{:S(2)}) collective-permute-start(f32[1,56,2560]{2,1,0:T(8,128)S(1)} %broadcast_select_fusion.27), channel_id=20, source_target_pairs={{0,15},{1,0},{2,1},{3,2},{4,3},{5,4},{6,5},{7,6},{8,7},{9,8},{10,9... | collective-permute-start | bytes 1720328 | tf_op jit(solution)/vmap(transpose(jvp()))/dot_general | solution.py:20
  1298.6 16.5 %collective-permute-start.6 = (f32[1,56,2560]{2,1,0:T(8,128)S(1)}, f32[1,56,2560]{2,1,0:T(8,128)S(1)}, u32[]{:S(2)}, u32[]{:S(2)}) collective-permute-start(f32[1,56,2560]{2,1,0:T(8,128)S(1)} %get-tuple-element.471), channel_id=23, source_target_pairs={{0,1},{1,2},{2,3},{3,4},{4,5},{5,6},{6,7},{7,8},{8,9},{9,10},{10,1... | collective-permute-start | bytes 1720328 | tf_op jit(solution)/vmap(transpose(jvp()))/dot_general | solution.py:20
  1315.9 30.9 %collective-permute-start.27 = (f32[1,56,2560]{2,1,0:T(8,128)}, f32[1,56,2560]{2,1,0:T(8,128)}, u32[]{:S(2)}, u32[]{:S(2)}) collective-permute-start(f32[1,56,2560]{2,1,0:T(8,128)} %copy-done.32), channel_id=36, source_target_pairs={{0,1},{1,2},{2,3},{3,4},{4,5},{5,6},{6,7},{7,8},{8,9},{9,10},{10,1... | collective-permute-start | bytes 1720328 | tf_op jit(solution)/vmap(transpose(jvp()))/dot_general | solution.py:21
  1332.7 18.2 %collective-permute-start.24 = (f32[1,56,2560]{2,1,0:T(8,128)}, f32[1,56,2560]{2,1,0:T(8,128)S(1)}, u32[]{:S(2)}, u32[]{:S(2)}) collective-permute-start(f32[1,56,2560]{2,1,0:T(8,128)} %copy-done.30), channel_id=18, source_target_pairs={{0,1},{1,2},{2,3},{3,4},{4,5},{5,6},{6,7},{7,8},{8,9},{9,10},{10,1... | collective-permute-start | bytes 1720328 | tf_op jit(solution)/vmap(transpose(jvp()))/dot_general | solution.py:20
  1333.5 17.4 %collective-permute-start.25 = (f32[1,56,2560]{2,1,0:T(8,128)}, f32[1,56,2560]{2,1,0:T(8,128)S(1)}, u32[]{:S(2)}, u32[]{:S(2)}) collective-permute-start(f32[1,56,2560]{2,1,0:T(8,128)} %copy-done.28), channel_id=24, source_target_pairs={{0,1},{1,2},{2,3},{3,4},{4,5},{5,6},{6,7},{7,8},{8,9},{9,10},{10,1... | collective-permute-start | bytes 1720328 | tf_op jit(solution)/vmap(transpose(jvp()))/dot_general | solution.py:20
  (111 other events, 2560.7 us)
Sparse Core Ops, SparseCore 0:
  10.3 54.8 all-gather.29
  67.5 51.1 all-gather.31
  121.0 51.1 all-gather.33
  174.4 51.1 all-gather.35
  227.8 51.1 all-gather.39
  281.2 51.1 all-gather.37
where the time goes:
time: 1380 us; the launch traced here: 1360 us
  waiting for transfers between devices  511 us (37%)
  matrix products  405 us (29%)
  starting transfers between devices  233 us (17%)
  local copies, waits for them, and re-layouts  85.7 us (6%)
  other arithmetic  61 us (4%)
  loops' own time  47.2 us (3%)
  between operations  15.1 us (1%)
    squeeze x6, waiting for transfers between devices, stack(): h = layer(h, {name: w[number] for name, w in weights.items()})  160 us
    dot_general x20, matrix products, layer(): up = jnp.dot(a, w['w_up'], preferred_element_type=jnp.float32)  144 us
    dot_general x19, matrix products, matmul(): jnp.dot(a, w, preferred_element_type=jnp.float32).astype(jnp.bfloat16)  135 us
    dot_general x20, matrix products, layer(): gate = jnp.dot(a, w['w_gate'], preferred_element_type=jnp.float32)  126 us
    dot_general x34, waiting for transfers between devices, layer(): gate = jnp.dot(a, w['w_gate'], preferred_element_type=jnp.float32)  121 us
    dot_general x34, waiting for transfers between devices, layer(): up = jnp.dot(a, w['w_up'], preferred_element_type=jnp.float32)  118 us
    dot_general x34, waiting for transfers between devices, matmul(): jnp.dot(a, w, preferred_element_type=jnp.float32).astype(jnp.bfloat16)  111 us
    dot_general x34, starting transfers between devices, layer(): gate = jnp.dot(a, w['w_gate'], preferred_element_type=jnp.float32)  85.3 us
  transfers between devices with their start and end apart: 108, of which 66 were waited for; matrix products, arithmetic and copies ran while one was open for 40% of the time, Pallas kernels for 0%

commit v1 on v0

v1 whole, which is shorter than its diff:
```python
import functools

import jax
import jax.numpy as jnp
from jax import lax
from jax.experimental import pallas as pl
from jax.experimental.pallas import tpu as pltpu
from jax.sharding import PartitionSpec as P

BF16, F32 = jnp.bfloat16, jnp.float32
ANY = pl.BlockSpec(memory_space=pl.ANY)
VMEM_LIMIT = 62 * 1024 * 1024
NY, NZ = 2, 4
TOKENS, CHUNK = 512, 512


def device(y, z, c):
    return (y * NZ + z) * 2 + c


class Place:
    def __init__(self):
        self.me = lax.axis_index("dp")
        self.c = lax.rem(self.me, 2)
        self.z = lax.rem(lax.div(self.me, 2), NZ)
        self.y = lax.div(self.me, 2 * NZ)
        self.y_mate = device(1 - self.y, self.z, self.c)
        self.sibling = device(self.y, self.z, 1 - self.c)

    def ahead(self, d):
        return lax.rem(self.z + d, NZ)

    def behind(self, d):
        return lax.rem(self.z + NZ - d, NZ)

    def z_mate(self, d):
        return device(self.y, self.ahead(d), self.c)

    def greet(self):
        barrier = pltpu.get_barrier_semaphore()
        mates = [self.z_mate(d) for d in (1, 2, 3)] + [self.y_mate, self.sibling]
        for mate in mates:
            pl.semaphore_signal(barrier, inc=1, device_id={"dp": mate}, device_id_type=pl.DeviceIdType.MESH)
        pl.semaphore_wait(barrier, len(mates))


def remote(src, dst, send, recv, to):
    return pltpu.make_async_remote_copy(
        src_ref=src, dst_ref=dst, send_sem=send, recv_sem=recv, device_id={"dp": to}, device_id_type=pl.DeviceIdType.MESH
    )


class Gather:
    def __init__(self, place, src, out, stage, send, recv, local):
        self.p, self.src, self.out, self.stage, self.send, self.recv, self.local = place, src, out, stage, send, recv, local
        self.rows = src.shape[0]

    def block(self, j):
        return self.out.at[pl.ds(pl.multiple_of(j * self.rows, 8), self.rows), :]

    def copy(self, src, dst, slot, to):
        return remote(src, dst, self.send.at[slot], self.recv.at[slot], to)

    def begin(self):
        p, mine = self.p, self.block(self.p.me)
        for d in (1, 2, 3):
            self.copy(self.src, mine, d - 1, p.z_mate(d)).start()
        self.copy(self.src, mine, 3, p.y_mate).start()
        self.copy(self.src, mine, 7, p.sibling).start()
        own = pltpu.make_async_copy(self.src, self.stage, self.local.at[0])
        own.start()
        own.wait()
        pltpu.make_async_copy(self.stage, mine, self.local.at[1]).start()

    def from_z(self, d):
        p = self.p
        block = self.block(device(p.y, p.behind(d), p.c))
        self.copy(block, block, d - 1, p.y_mate).wait_recv()
        self.copy(block, block, 3 + d, p.y_mate).start()
        self.copy(block, block, 7 + d, p.sibling).start()

    def from_y(self, d):
        p = self.p
        block = self.block(device(1 - p.y, p.behind(d), p.c))
        self.copy(block, block, 3 + d, p.y_mate).wait_recv()
        self.copy(block, block, 11 + d, p.sibling).start()

    def finish(self):
        p = self.p
        for k in range(8):
            row = p.y if k < 4 else 1 - p.y
            block = self.block(device(row, p.behind(k % 4), 1 - p.c))
            self.copy(block, block, 7 + k, p.sibling).wait_recv()
        mine = self.block(p.me)
        for slot in range(15):
            self.copy(mine, mine, slot, p.sibling).wait_send()
        pltpu.make_async_copy(self.stage, mine, self.local.at[1]).wait()

    @staticmethod
    def scratch(shape):
        return [pltpu.VMEM(shape, BF16), pltpu.SemaphoreType.DMA((15,)), pltpu.SemaphoreType.DMA((15,)), pltpu.SemaphoreType.DMA((2,))]


class Scatter:
    def __init__(self, place, src, out, own, sib, from_y, from_z, total, send, recv, local):
        self.p, self.src, self.out, self.total = place, src, out, total
        self.own, self.sib, self.y_slots, self.z_slots = own, sib, from_y, from_z
        self.send, self.recv, self.local = send, recv, local
        self.rows = out.shape[0]

    def block(self, k, c):
        row = 1 - self.p.y if k < 4 else self.p.y
        j = device(row, self.p.ahead(k % 4), c)
        return self.src.at[pl.ds(pl.multiple_of(j * self.rows, 8), self.rows), :]

    def to_sibling(self, k):
        return remote(self.block(k, 1 - self.p.c), self.sib.at[k], self.send.at[k], self.recv.at[k], self.p.sibling)

    def to_y(self, d):
        return remote(self.own.at[d], self.y_slots.at[d], self.send.at[8 + d], self.recv.at[8 + d], self.p.y_mate)

    def to_z(self, d):
        return remote(self.own.at[4 + d], self.z_slots.at[d - 1], self.send.at[11 + d], self.recv.at[11 + d], self.p.z_mate(d))

    def load(self, k):
        return pltpu.make_async_copy(self.block(k, self.p.c), self.own.at[k], self.local.at[k])

    def begin(self):
        for k in (1, 2, 3, 0, 5, 6, 7, 4):
            self.to_sibling(k).start()
            self.load(k).start()

    def add(self, refs, to):
        rows, columns = self.rows, self.own.shape[2]
        if columns % 512 == 0:
            count, at = columns // 256, lambda i: (slice(None), pl.ds(pl.multiple_of(i * 256, 256), 256))
        else:
            count, at = rows // 16, lambda i: (pl.ds(pl.multiple_of(i * 16, 16), 16), slice(None))

        def some(i, carry):
            here = at(i)
            value = refs[0][here].astype(F32)
            for ref in refs[1:]:
                value = value + ref[here].astype(F32)
            to[here] = value.astype(BF16)
            return carry

        lax.fori_loop(0, count, some, 0)

    def send_y(self, d):
        self.load(d).wait()
        self.to_sibling(d).wait_recv()
        self.add((self.own.at[d], self.sib.at[d]), self.own.at[d])
        self.to_y(d).start()

    def send_z(self, d):
        self.load(4 + d).wait()
        self.to_sibling(4 + d).wait_recv()
        self.to_y(d).wait_recv()
        self.add((self.own.at[4 + d], self.sib.at[4 + d], self.y_slots.at[d]), self.own.at[4 + d])
        self.to_z(d).start()

    def finish(self):
        self.load(4).wait()
        self.to_sibling(4).wait_recv()
        self.to_y(0).wait_recv()
        for d in (1, 2, 3):
            self.to_z(d).wait_recv()
        self.add([self.own.at[4], self.sib.at[4], self.y_slots.at[0]] + [self.z_slots.at[d] for d in range(3)], self.total)
        store = pltpu.make_async_copy(self.total, self.out, self.local.at[8])
        store.start()
        for k in range(8):
            self.to_sibling(k).wait_send()
        for d in range(4):
            self.to_y(d).wait_send()
        for d in (1, 2, 3):
            self.to_z(d).wait_send()
        store.wait()

    @staticmethod
    def scratch(shape):
        return [pltpu.VMEM((n, *shape), BF16) for n in (8, 8, 4, 3)] + [
            pltpu.VMEM(shape, BF16),
            pltpu.SemaphoreType.DMA((15,)),
            pltpu.SemaphoreType.DMA((15,)),
            pltpu.SemaphoreType.DMA((9,)),
        ]


def gather_events(jobs):
    events = []
    for n in range(len(jobs) + 1):
        if n < len(jobs):
            events += [functools.partial(jobs[n].from_z, d) for d in (1, 2, 3)]
        if n > 0:
            events += [functools.partial(jobs[n - 1].from_y, d) for d in (0, 1, 2, 3)]
    return events + [job.finish for job in jobs]


def scatter_events(jobs):
    events = []
    for n in range(len(jobs) + 2):
        if n < len(jobs):
            events += [functools.partial(jobs[n].send_y, d) for d in (1, 2, 3, 0)]
        if 0 < n <= len(jobs):
            events += [functools.partial(jobs[n - 1].send_z, d) for d in (1, 2, 3)]
        if n > 1:
            events.append(jobs[n - 2].finish)
    return events


def spread(events, steps):
    by_step = [[] for _ in range(steps)]
    for n, event in enumerate(events):
        by_step[n * steps // len(events)].append(event)
    return by_step


def at_step(by_step, step):
    for n, events in enumerate(by_step):
        if events:

            @pl.when(step == n)
            def _(events=events):
                for event in events:
                    event()


def dot(a, b, contract):
    return lax.dot_general(a, b, (contract, ((), ())), preferred_element_type=F32)


def scale_of(wide):
    return lax.rsqrt(jnp.mean(wide * wide, -1, keepdims=True) + 1e-6)


def forward(h, wg, wu, wd, out, a, acc, hook):
    tokens, dim = h.shape
    tiles, chunks = tokens // TOKENS, wg.shape[1] // CHUNK

    def body(h, wg, wu, wd, out):
        t, f = pl.program_id(0), pl.program_id(1)
        hook(t * chunks + f)

        @pl.when(f == 0)
        def _():
            wide = h[...].astype(F32)
            a[...] = (wide * scale_of(wide)).astype(BF16)
            acc[...] = jnp.zeros_like(acc)

        gate = dot(a[...], wg[...], ((1,), (0,)))
        up = dot(a[...], wu[...], ((1,), (0,)))
        hid = (gate * jax.nn.sigmoid(gate) * up).astype(BF16)
        acc[...] += dot(hid, wd[...], ((1,), (0,)))

        @pl.when(f == chunks - 1)
        def _():
            out[...] = (h[...].astype(F32) + acc[...].astype(BF16).astype(F32)).astype(BF16)

    whole = pl.BlockSpec((TOKENS, dim), lambda t, f: (t, 0))
    pltpu.emit_pipeline(
        body,
        grid=(tiles, chunks),
        in_specs=[
            whole,
            pl.BlockSpec((dim, CHUNK), lambda t, f: (0, f)),
            pl.BlockSpec((dim, CHUNK), lambda t, f: (0, f)),
            pl.BlockSpec((CHUNK, dim), lambda t, f: (f, 0)),
        ],
        out_specs=[whole],
    )(h, wg, wu, wd, out)


def backward(h, dy, wg, wu, wd, dh, a, hid, dgate, dup, acc, hook):
    tokens, dim = h.shape
    tiles, chunks = tokens // TOKENS, wg.shape[1] // CHUNK

    def body(h, dy, wg, wu, wd, dh, a, hid, dgate, dup):
        t, f = pl.program_id(0), pl.program_id(1)
        hook(t * chunks + f)

        @pl.when(f == 0)
        def _():
            wide = h[...].astype(F32)
            a[...] = (wide * scale_of(wide)).astype(BF16)
            acc[...] = jnp.zeros_like(acc)

        gate = dot(a[...], wg[...], ((1,), (0,)))
        up = dot(a[...], wu[...], ((1,), (0,)))
        dhid = dot(dy[...], wd[...], ((1,), (1,))).astype(BF16).astype(F32)
        s = jax.nn.sigmoid(gate)
        silu = gate * s
        hid[...] = (silu * up).astype(BF16)
        by_gate = (dhid * up * (s * (1 + gate * (1 - s)))).astype(BF16)
        by_up = (dhid * silu).astype(BF16)
        dgate[...] = by_gate
        dup[...] = by_up
        acc[...] += dot(by_gate, wg[...], ((1,), (1,))) + dot(by_up, wu[...], ((1,), (1,)))

        @pl.when(f == chunks - 1)
        def _():
            wide = h[...].astype(F32)
            scale = scale_of(wide)
            da = acc[...].astype(BF16).astype(F32)
            along = jnp.mean(da * wide, -1, keepdims=True)
            by_h = (da * scale - wide * (along * scale * scale * scale)).astype(BF16)
            dh[...] = (dy[...].astype(F32) + by_h.astype(F32)).astype(BF16)

    whole = pl.BlockSpec((TOKENS, dim), lambda t, f: (t, 0))
    part = pl.BlockSpec((TOKENS, CHUNK), lambda t, f: (t, f))
    pltpu.emit_pipeline(
        body,
        grid=(tiles, chunks),
        in_specs=[
            whole,
            whole,
            pl.BlockSpec((dim, CHUNK), lambda t, f: (0, f)),
            pl.BlockSpec((dim, CHUNK), lambda t, f: (0, f)),
            pl.BlockSpec((CHUNK, dim), lambda t, f: (f, 0)),
        ],
        out_specs=[whole, whole, part, part, part],
    )(h, dy, wg, wu, wd, dh, a, hid, dgate, dup)


def by_weights(a, dy, hid, dgate, dup, dwg, dwu, dwd, hook):
    tokens, dim = a.shape
    chunks = hid.shape[1] // CHUNK

    def body(a, dy, hid, dgate, dup, dwg, dwu, dwd):
        hook(pl.program_id(0))
        dwd[...] = dot(hid[...], dy[...], ((0,), (0,))).astype(BF16)
        dwg[...] = dot(a[...], dgate[...], ((0,), (0,))).astype(BF16)
        dwu[...] = dot(a[...], dup[...], ((0,), (0,))).astype(BF16)

    whole = pl.BlockSpec((tokens, dim), lambda f: (0, 0))
    part = pl.BlockSpec((tokens, CHUNK), lambda f: (0, f))
    wide = pl.BlockSpec((dim, CHUNK), lambda f: (0, f))
    pltpu.emit_pipeline(
        body,
        grid=(chunks,),
        in_specs=[whole, whole, part, part, part],
        out_specs=[wide, wide, pl.BlockSpec((CHUNK, dim), lambda f: (f, 0))],
    )(a, dy, hid, dgate, dup, dwg, dwu, dwd)


def nothing(step):
    pass


def call(body, outs, scratch, collective, *args):
    return pl.pallas_call(
        body,
        out_shape=[jax.ShapeDtypeStruct(shape, BF16) for shape in outs],
        in_specs=[ANY] * len(args),
        out_specs=[ANY] * len(outs),
        scratch_shapes=scratch,
        compiler_params=pltpu.CompilerParams(collective_id=collective, has_side_effects=True, vmem_limit_bytes=VMEM_LIMIT)
        if collective is not None
        else pltpu.CompilerParams(vmem_limit_bytes=VMEM_LIMIT),
    )(*args)


def solution(mesh):
    def step(x, dy, *weights):
        tokens, dim = x.shape[1:]
        ff = weights[0].shape[2]
        x, dy = x[0], dy[0]
        shards = [w.shape[1:] for w in weights]
        wholes = [(16 * r, c) for r, c in shards]
        n_gather, n_scatter = len(Gather.scratch((8, 128))), len(Scatter.scratch((8, 128)))
        gather_scratch = [s for shape in shards for s in Gather.scratch(shape)]
        scatter_scratch = [s for shape in shards for s in Scatter.scratch(shape)]

        def gathers(n, place, srcs, outs, scratch):
            return [Gather(place, srcs[i].at[n], outs[i], *scratch[n_gather * i : n_gather * (i + 1)]) for i in range(3)]

        def scatters(place, srcs, outs, scratch):
            return [Scatter(place, srcs[i], outs[i], *scratch[n_scatter * i : n_scatter * (i + 1)]) for i in range(3)]

        def k1(*refs):
            place = Place()
            place.greet()
            jobs = gathers(0, place, refs[:3], refs[3:6], refs[6:])
            for job in jobs:
                job.begin()
            for event in gather_events(jobs):
                event()

        first = call(k1, wholes, gather_scratch, 1, *weights)

        def k2(*refs):
            h, wg, wu, wd = refs[:4]
            place = Place()
            place.greet()
            out = refs[7]
            jobs = gathers(1, place, refs[4:7], refs[8:11], refs[13:])
            for job in jobs:
                job.begin()
            steps = (tokens // TOKENS) * (ff // CHUNK)
            by_step = spread(gather_events(jobs), steps)
            forward(h, wg, wu, wd, out, refs[11], refs[12], functools.partial(at_step, by_step))

        tile = [pltpu.VMEM((TOKENS, dim), BF16), pltpu.VMEM((TOKENS, dim), F32)]
        h1, *second = call(k2, [(tokens, dim), *wholes], tile + gather_scratch, 2, x, *first, *weights)

        acc = [pltpu.VMEM((TOKENS, dim), F32)]
        saved = [(tokens, dim), (tokens, dim), (tokens, ff), (tokens, ff), (tokens, ff)]

        def k3(*refs):
            h, dy, wg, wu, wd, dh, a, hid, dgate, dup, dwg, dwu, dwd, acc = refs
            backward(h, dy, wg, wu, wd, dh, a, hid, dgate, dup, acc, nothing)
            by_weights(a, dy, hid, dgate, dup, dwg, dwu, dwd, nothing)

        d1, _, _, _, _, *terms1 = call(k3, saved + wholes, acc, None, h1, dy, *second)

        def k4(*refs):
            h, dy, wg, wu, wd = refs[:5]
            terms = refs[5:8]
            dh, a, hid, dgate, dup, dwg, dwu, dwd = refs[8:16]
            outs = refs[16:19]
            acc = refs[19]
            place = Place()
            place.greet()
            jobs = scatters(place, terms, outs, refs[20:])
            for job in jobs:
                job.begin()
            steps = (tokens // TOKENS) * (ff // CHUNK)
            by_step = spread(scatter_events(jobs), steps + 5)
            backward(h, dy, wg, wu, wd, dh, a, hid, dgate, dup, acc, functools.partial(at_step, by_step[:steps]))
            by_weights(a, dy, hid, dgate, dup, dwg, dwu, dwd, functools.partial(at_step, by_step[steps:]))

        d0, _, _, _, _, *rest = call(k4, saved + wholes + shards, acc + scatter_scratch, 3, x, d1, *first, *terms1)
        terms0, sums1 = rest[:3], rest[3:]

        def k5(*refs):
            place = Place()
            place.greet()
            jobs = scatters(place, refs[:3], refs[3:6], refs[6:])
            for job in jobs:
                job.begin()
            for event in scatter_events(jobs):
                event()

        sums0 = call(k5, shards, scatter_scratch, 4, *terms0)
        return (d0[None], *(jnp.stack(pair) for pair in zip(sums0, sums1)))

    tokens, rows, out = P(("rep", "dp")), P(None, "dp"), P("rep", "dp")
    return jax.shard_map(
        step, mesh=mesh, in_specs=(tokens, tokens, rows, rows, rows), out_specs=(tokens, out, out, out), check_vma=False
    )
```

time: 1380 us -> 547 us (0.40); the launches traced: 1360 us -> 547 us
  Pallas kernels: 0 us -> 538 us
  waiting for transfers between devices: 511 us -> 0 us
  matrix products: 405 us -> 0 us
  starting transfers between devices: 233 us -> 0 us
  local copies, waits for them, and re-layouts: 85.7 us -> 4.18 us
  other arithmetic: 61 us -> 3.98 us
  loops' own time: 47.2 us -> 0 us
  between operations: 15.1 us -> 0.7 us
    pallas_call x0 -> x5, Pallas kernels: none -> 538 us  [call(): pl.pallas_call(body, out_shape=[jax.ShapeDtypeStruct(shape, BF16) for sha...]
    dot_general x59 -> x0, matrix products: 405 us -> none  [the longest x20 144 us: layer(): up = jnp.dot(a, w['w_up'], preferred_element_type=jnp.float32)]
    dot_general x102 -> x0, waiting for transfers between devices: 350 us -> none  [the longest x34 121 us: layer(): gate = jnp.dot(a, w['w_gate'], preferred_element_type=jnp.float32)]
    dot_general x102 -> x0, starting transfers between devices: 233 us -> none  [the longest x34 85.3 us: layer(): gate = jnp.dot(a, w['w_gate'], preferred_element_type=jnp.float32)]
    squeeze x6 -> x0, waiting for transfers between devices: 160 us -> none  [stack(): h = layer(h, {name: w[number] for name, w in weights.items()})]
    unnamed x77 -> x7, local copies, waits for them, and re-layouts: 65.2 us -> 4.18 us
    another operation x6 -> x0, loops' own time: 47.2 us -> none  [the longest x2 16.4 us: layer(): up = jnp.dot(a, w['w_up'], preferred_element_type=jnp.float32)]
    dot_general x96 -> x0, other arithmetic: 34.5 us -> none
  transfers between devices with their start and end apart: 108 -> 0, of which waited for: 66 -> 0; matrix products, arithmetic and copies ran while one was open for 40% -> 0% of each run, Pallas kernels for 0% -> 0%
where the time goes in v1:
time: 547 us
  Pallas kernels  538 us (98%)
    pallas_call x5, Pallas kernels, call(): pl.pallas_call(body, out_shape=[jax.ShapeDtypeStruct(shape, BF16) for sha...  538 us

profile of v1, /device:TPU:0, one launch (start us, length us, event | category | flops | bytes accessed | tf_op | source)
XLA Modules:
  0.0 546.8 jit_solution(16138695891980760542)
XLA Ops:
  0.6 96.0 %shard_map.84 = (bf16[896,2560]{1,0:T(8,128)(2,1)}, bf16[896,2560]{1,0:T(8,128)(2,1)}, bf16[2560,896]{1,0:T(8,128)(2,1)}) custom-call(bf16[2,56,2560]{2,1,0:T(8,128)(2,1)} %refs_4_.1, bf16[2,56,2560]{2,1,0:T(8,128)(2,1)} %refs_5_.1, bf16[2,160,896]{2,1,0:T(8,128)(2,1)} %refs_6_.1), custom_call_target="tpu_custom_call" | custom-call | tf_op jit(solution)/shard_map/pallas_call | solution.py:351
  96.6 108.4 %shard_map.85 = (bf16[2048,896]{1,0:T(8,128)(2,1)}, bf16[896,2560]{1,0:T(8,128)(2,1)}, bf16[896,2560]{1,0:T(8,128)(2,1)}, bf16[2560,896]{1,0:T(8,128)(2,1)}) custom-call(bf16[2048,896]{1,0:T(8,128)(2,1)} %bitcast.9, bf16[896,2560]{1,0:T(8,128)(2,1)} %get-tuple-element.25.refs_1_.refs_2_, bf16[896,2560]{1,0:T(8,128)(2,1)} %get-tuple-element.26.refs_2_.refs_3_, ...), custom_call_target="tpu_custom_call" | custom-call | tf_op jit(solution)/shard_map/pallas_call | solution.py:351
  205.0 110.7 %shard_map.86 = (bf16[2048,896]{1,0:T(8,128)(2,1)}, bf16[2048,896]{1,0:T(8,128)(2,1)}, bf16[2048,2560]{1,0:T(8,128)(2,1)}, bf16[2048,2560]{1,0:T(8,128)(2,1)}, b...) custom-call(bf16[2048,896]{1,0:T(8,128)(2,1)} %get-tuple-element.28., ...), custom_call_target="tpu_custom_call" | custom-call | tf_op jit(solution)/shard_map/pallas_call | solution.py:351
  315.8 132.9 %shard_map.87 = (bf16[2048,896]{1,0:T(8,128)(2,1)}, bf16[2048,896]{1,0:T(8,128)(2,1)}, bf16[2048,2560]{1,0:T(8,128)(2,1)}, bf16[2048,2560]{1,0:T(8,128)(2,1)}, b...) custom-call(bf16[2048,896]{1,0:T(8,128)(2,1)} %bitcast.10, ...), custom_call_target="tpu_custom_call" | custom-call | tf_op jit(solution)/shard_map/pallas_call | solution.py:351
  448.7 0.0 copy-start
  448.7 0.0 copy-start.1
  448.7 0.0 copy-start.2
  448.7 89.9 %shard_map.88 = (bf16[56,2560]{1,0:T(8,128)(2,1)}, bf16[56,2560]{1,0:T(8,128)(2,1)}, bf16[160,896]{1,0:T(8,128)(2,1)}) custom-call(bf16[896,2560]{1,0:T(8,128)(2,1)} %get-tuple-element.37.refs_0_, bf16[896,2560]{1,0:T(8,128)(2,1)} %get-tuple-element.38.refs_1_, bf16[2560,896]{1,0:T(8,128)(2,1)} %get-tuple-element.39.refs_2_), custom_call_target="tpu_custom_call" | custom-call | tf_op jit(solution)/shard_map/pallas_call | solution.py:351
  538.6 0.0 copy-done
  538.6 0.0 copy-done.1
  538.6 2.1 pad_maximum_fusion
  540.8 0.0 copy-done.2
  540.8 1.8 pad_maximum_fusion.2
  542.6 4.2 copy.10
Async XLA Ops:
  448.7 89.9 %copy-start = (bf16[56,2560]{1,0:T(8,128)(2,1)S(1)}, bf16[56,2560]{1,0:T(8,128)(2,1)}, u32[]{:S(2)}) copy-start(bf16[56,2560]{1,0:T(8,128)(2,1)} %get-tuple-element.41) | copy-start | bytes 860164
  448.7 89.9 %copy-start.1 = (bf16[56,2560]{1,0:T(8,128)(2,1)S(1)}, bf16[56,2560]{1,0:T(8,128)(2,1)}, u32[]{:S(2)}) copy-start(bf16[56,2560]{1,0:T(8,128)(2,1)} %get-tuple-element.43) | copy-start | bytes 860164
  448.7 92.1 %copy-start.2 = (bf16[160,896]{1,0:T(8,128)(2,1)S(1)}, bf16[160,896]{1,0:T(8,128)(2,1)}, u32[]{:S(2)}) copy-start(bf16[160,896]{1,0:T(8,128)(2,1)} %get-tuple-element.45) | copy-start | bytes 860164

commit v2 on v1

v2 whole, which is shorter than its diff:
```python
import functools

import jax
import jax.numpy as jnp
from jax import lax
from jax.experimental import pallas as pl
from jax.experimental.pallas import tpu as pltpu
from jax.sharding import PartitionSpec as P

BF16, F32 = jnp.bfloat16, jnp.float32
ANY = pl.BlockSpec(memory_space=pl.ANY)
VMEM_LIMIT = 66_500_000
NY, NZ = 2, 4
TOKENS, TILE, CHUNK, RING = 512, 1024, 256, 4


def device(y, z, c):
    return (y * NZ + z) * 2 + c


class Place:
    def __init__(self):
        self.me, self.x = lax.axis_index("dp"), lax.axis_index("rep")
        self.c = lax.rem(self.me, 2)
        self.z = lax.rem(lax.div(self.me, 2), NZ)
        self.y = lax.div(self.me, 2 * NZ)
        self.y_mate = device(1 - self.y, self.z, self.c)
        self.sibling = device(self.y, self.z, 1 - self.c)

    def ahead(self, d):
        return lax.rem(self.z + d, NZ)

    def behind(self, d):
        return lax.rem(self.z + NZ - d, NZ)

    def z_mate(self, d):
        return device(self.y, self.ahead(d), self.c)

    def greet(self, across):
        barrier = pltpu.get_barrier_semaphore()
        mates = [{"dp": self.z_mate(d)} for d in (1, 2, 3)] + [{"dp": self.y_mate}, {"dp": self.sibling}]
        if across:
            mates.append({"rep": 1 - self.x})
        for mate in mates:
            pl.semaphore_signal(barrier, inc=1, device_id=mate, device_id_type=pl.DeviceIdType.MESH)
        pl.semaphore_wait(barrier, len(mates))


def remote(src, dst, send, recv, to):
    return pltpu.make_async_remote_copy(
        src_ref=src, dst_ref=dst, send_sem=send, recv_sem=recv, device_id=to if isinstance(to, dict) else {"dp": to}, device_id_type=pl.DeviceIdType.MESH
    )


class Gather:
    def __init__(self, place, src, out, stage, send, recv, local):
        self.p, self.src, self.out, self.stage, self.send, self.recv, self.local = place, src, out, stage, send, recv, local
        self.rows, self.columns = src.shape
        self.across = {"rep": 1 - place.x}

    def block(self, j):
        return self.out.at[pl.ds(pl.multiple_of(j * self.rows, 8), self.rows), :]

    def half(self, ref, first, x):
        if self.columns % 512 == 0:
            size = self.columns // 2
            return ref.at[pl.ds(pl.multiple_of(first, 8), self.rows), pl.ds(pl.multiple_of(x * size, size), size)]
        size = self.rows // 2
        return ref.at[pl.ds(pl.multiple_of(first + x * size, 8), size), :]

    def part(self, j, x):
        return self.half(self.out, j * self.rows, x)

    def copy(self, src, dst, slot, to):
        return remote(src, dst, self.send.at[slot], self.recv.at[slot], to)

    def begin(self):
        p, mine = self.p, self.block(self.p.me)
        for d in (1, 2, 3):
            if d == 1:
                self.copy(self.src, mine, 0, p.z_mate(d)).start()
            else:
                self.copy(self.half(self.src, 0, p.x), self.part(p.me, p.x), d - 1, p.z_mate(d)).start()
        self.copy(self.src, mine, 3, p.y_mate).start()
        self.copy(self.src, mine, 13, p.sibling).start()
        pltpu.make_async_copy(self.src, self.stage, self.local.at[0]).start()

    def keep(self):
        pltpu.make_async_copy(self.src, self.stage, self.local.at[0]).wait()
        pltpu.make_async_copy(self.stage, self.block(self.p.me), self.local.at[1]).start()

    def from_z(self, d):
        p = self.p
        j = device(p.y, p.behind(d), p.c)
        block, part = self.block(j), self.part(j, p.x)
        if d == 1:
            self.copy(block, block, 0, p.y_mate).wait_recv()
            self.copy(block, block, 14, p.sibling).start()
        else:
            self.copy(part, part, d - 1, p.y_mate).wait_recv()
            self.copy(part, part, 6 + d, self.across).start()
        self.copy(part, part, 3 + d, p.y_mate).start()

    def from_across(self, d):
        p = self.p
        j = device(p.y, p.behind(d), p.c)
        part = self.part(j, 1 - p.x)
        self.copy(part, part, 6 + d, self.across).wait_recv()
        self.copy(self.block(j), self.block(j), 13 + d, p.sibling).start()

    def from_y(self, d):
        p = self.p
        j = device(1 - p.y, p.behind(d), p.c)
        if d == 0:
            block = self.block(j)
            self.copy(block, block, 3, p.y_mate).wait_recv()
            self.copy(block, block, 17, p.sibling).start()
        else:
            part = self.part(j, p.x)
            self.copy(part, part, 3 + d, p.y_mate).wait_recv()
            self.copy(part, part, 9 + d, self.across).start()

    def from_far(self, d):
        p = self.p
        j = device(1 - p.y, p.behind(d), p.c)
        part = self.part(j, 1 - p.x)
        self.copy(part, part, 9 + d, self.across).wait_recv()
        self.copy(self.block(j), self.block(j), 17 + d, p.sibling).start()

    def finish(self):
        p = self.p
        for k in range(8):
            row = p.y if k < 4 else 1 - p.y
            block = self.block(device(row, p.behind(k % 4), 1 - p.c))
            self.copy(block, block, 13 + k, p.sibling).wait_recv()
        mine, part = self.block(p.me), self.part(p.me, p.x)
        for slot in (n for n in range(21) if n != 7):
            sent = mine if slot in (0, 3) or slot >= 13 else part
            self.copy(sent, sent, slot, p.sibling).wait_send()
        pltpu.make_async_copy(self.stage, mine, self.local.at[1]).wait()

    @staticmethod
    def scratch(shape):
        return [pltpu.VMEM(shape, BF16), pltpu.SemaphoreType.DMA((21,)), pltpu.SemaphoreType.DMA((21,)), pltpu.SemaphoreType.DMA((2,))]


class Scatter:
    def __init__(self, place, src, out, own, sib, from_y, from_z, total, send, recv, local):
        self.p, self.src, self.out, self.total = place, src, out, total
        self.own, self.sib, self.y_slots, self.z_slots = own, sib, from_y, from_z
        self.send, self.recv, self.local = send, recv, local
        self.rows = out.shape[0]

    def block(self, k, c):
        row = 1 - self.p.y if k < 4 else self.p.y
        j = device(row, self.p.ahead(k % 4), c)
        return self.src.at[pl.ds(pl.multiple_of(j * self.rows, 8), self.rows), :]

    def to_sibling(self, k):
        return remote(self.block(k, 1 - self.p.c), self.sib.at[k], self.send.at[k], self.recv.at[k], self.p.sibling)

    def to_y(self, d):
        return remote(self.own.at[d], self.y_slots.at[d], self.send.at[8 + d], self.recv.at[8 + d], self.p.y_mate)

    def to_z(self, d):
        return remote(self.own.at[4 + d], self.z_slots.at[d - 1], self.send.at[11 + d], self.recv.at[11 + d], self.p.z_mate(d))

    def load(self, k):
        return pltpu.make_async_copy(self.block(k, self.p.c), self.own.at[k], self.local.at[k])

    def begin(self):
        for k in (1, 2, 3, 0, 5, 6, 7, 4):
            self.to_sibling(k).start()
            self.load(k).start()

    def add(self, refs, to):
        rows, columns = self.rows, self.own.shape[2]
        if columns % 512 == 0:
            count, at = columns // 256, lambda i: (slice(None), pl.ds(pl.multiple_of(i * 256, 256), 256))
        else:
            count, at = rows // 16, lambda i: (pl.ds(pl.multiple_of(i * 16, 16), 16), slice(None))

        def some(i, carry):
            here = at(i)
            value = refs[0][here].astype(F32)
            for ref in refs[1:]:
                value = value + ref[here].astype(F32)
            to[here] = value.astype(BF16)
            return carry

        lax.fori_loop(0, count, some, 0)

    def send_y(self, d):
        self.load(d).wait()
        self.to_sibling(d).wait_recv()
        self.add((self.own.at[d], self.sib.at[d]), self.own.at[d])
        self.to_y(d).start()

    def send_z(self, d):
        self.load(4 + d).wait()
        self.to_sibling(4 + d).wait_recv()
        self.to_y(d).wait_recv()
        self.add((self.own.at[4 + d], self.sib.at[4 + d], self.y_slots.at[d]), self.own.at[4 + d])
        self.to_z(d).start()

    def finish(self):
        self.load(4).wait()
        self.to_sibling(4).wait_recv()
        self.to_y(0).wait_recv()
        for d in (1, 2, 3):
            self.to_z(d).wait_recv()
        self.add([self.own.at[4], self.sib.at[4], self.y_slots.at[0]] + [self.z_slots.at[d] for d in range(3)], self.total)
        store = pltpu.make_async_copy(self.total, self.out, self.local.at[8])
        store.start()
        for k in range(8):
            self.to_sibling(k).wait_send()
        for d in range(4):
            self.to_y(d).wait_send()
        for d in (1, 2, 3):
            self.to_z(d).wait_send()
        store.wait()

    @staticmethod
    def scratch(shape):
        return [pltpu.VMEM((n, *shape), BF16) for n in (8, 8, 4, 3)] + [
            pltpu.VMEM(shape, BF16),
            pltpu.SemaphoreType.DMA((15,)),
            pltpu.SemaphoreType.DMA((15,)),
            pltpu.SemaphoreType.DMA((9,)),
        ]


class Stream:
    def __init__(self, place, outs, own, sib, from_y, from_z, total, send, recv, local):
        self.p, self.outs, self.total = place, outs, total
        self.own, self.sib, self.y_slots, self.z_slots = own, sib, from_y, from_z
        self.send, self.recv, self.local = send, recv, local
        self.rows, self.width = own.shape[5:]

    def mine(self, f, y):
        return self.own.at[lax.rem(f, RING), self.p.c, y]

    def copy(self, f, src, dst, slot, to):
        return remote(src, dst, self.send.at[f, slot], self.recv.at[f, slot], to)

    def to_sibling(self, f):
        return self.copy(f, self.own.at[lax.rem(f, RING), 1 - self.p.c], self.sib.at[f], 0, self.p.sibling)

    def to_y(self, f):
        return self.copy(f, self.mine(f, 1 - self.p.y), self.y_slots.at[f], 1, self.p.y_mate)

    def to_z(self, f, d):
        src = self.mine(f, self.p.y).at[self.p.ahead(d)]
        return self.copy(f, src, self.z_slots.at[f, d - 1], 1 + d, self.p.z_mate(d))

    def store(self, w, f, value):
        slot = lax.rem(f, RING)
        for j in range(16):
            y, z, c = j // 8, j // 2 % 4, j % 2
            self.own[slot, c, y, z, w] = value[j * self.rows : (j + 1) * self.rows].astype(BF16)

    def add(self, refs, to):
        for w in range(2):
            value = refs[0][w].astype(F32)
            for ref in refs[1:]:
                value = value + ref[w].astype(F32)
            to[w] = value.astype(BF16)

    def begin(self, f):
        self.to_sibling(f).start()

    def send_y(self, f):
        self.to_sibling(f).wait_recv()
        mine, sib = self.mine(f, 1 - self.p.y), self.sib.at[f, 1 - self.p.y]
        for z in range(NZ):
            self.add((mine.at[z], sib.at[z]), mine.at[z])
        self.to_y(f).start()

    def send_z(self, f):
        self.to_y(f).wait_recv()
        mine, sib, from_y = self.mine(f, self.p.y), self.sib.at[f, self.p.y], self.y_slots.at[f]
        for d in (1, 2, 3):
            z = self.p.ahead(d)
            self.add((mine.at[z], sib.at[z], from_y.at[z]), mine.at[z])
            self.to_z(f, d).start()

    def result(self, w, f):
        columns = pl.ds(pl.multiple_of(f * self.width, self.width), self.width)
        return pltpu.make_async_copy(self.total.at[f, w], self.outs[w].at[:, columns], self.local.at[f, w])

    def finish(self, f):
        for d in (1, 2, 3):
            self.to_z(f, d).wait_recv()
        terms = [t.at[self.p.z] for t in (self.mine(f, self.p.y), self.sib.at[f, self.p.y], self.y_slots.at[f])]
        self.add(terms + [self.z_slots.at[f, d] for d in range(3)], self.total.at[f])
        for w in range(2):
            self.result(w, f).start()
        self.to_sibling(f).wait_send()
        self.to_y(f).wait_send()
        for d in (1, 2, 3):
            self.to_z(f, d).wait_send()

    def close(self, runs):
        for f in range(runs):
            for w in range(2):
                self.result(w, f).wait()

    @staticmethod
    def scratch(shape):
        rows, columns = shape
        runs, block = columns // CHUNK, (2, rows, CHUNK)
        return [
            pltpu.VMEM((RING, 2, NY, NZ, *block), BF16),
            pltpu.VMEM((runs, NY, NZ, *block), BF16),
            pltpu.VMEM((runs, NZ, *block), BF16),
            pltpu.VMEM((runs, NZ - 1, *block), BF16),
            pltpu.VMEM((runs, *block), BF16),
            pltpu.SemaphoreType.DMA((runs, 5)),
            pltpu.SemaphoreType.DMA((runs, 5)),
            pltpu.SemaphoreType.DMA((runs, 2)),
        ]


def gather_events(jobs, first):
    rounds = []
    for n in range(len(jobs) + 2):
        events = []
        if n < len(jobs):
            events += [functools.partial(jobs[n].from_z, d) for d in (1, 2, 3)]
        if 0 < n <= len(jobs):
            for d in (0, 1, 2, 3):
                if d > 1:
                    events.append(functools.partial(jobs[n - 1].from_across, d))
                events.append(functools.partial(jobs[n - 1].from_y, d))
        if n > 1:
            events += [functools.partial(jobs[n - 2].from_far, d) for d in (1, 2, 3)]
        rounds.append(events)
    before, after = sum(rounds[: first + 2], []), sum(rounds[first + 2 :], [])
    return before + [job.finish for job in jobs[:first]], after + [job.finish for job in jobs[first:]]


def spread(events, steps):
    by_step = [[] for _ in range(steps)]
    for n, event in enumerate(events):
        by_step[n * steps // len(events)].append(event)
    return by_step


def at_step(by_step, step):
    for n, events in enumerate(by_step):
        if events:

            @pl.when(step == n)
            def _(events=events):
                for event in events:
                    event()


def dot(a, b, contract):
    return lax.dot_general(a, b, (contract, ((), ())), preferred_element_type=F32)


def scale_of(wide):
    return lax.rsqrt(jnp.mean(wide * wide, -1, keepdims=True) + 1e-6)


def forward(h, wg, wu, wd, out, hid, a, acc, hook):
    tokens, dim = h.shape
    width = 512
    tiles, chunks = tokens // TOKENS, wg.shape[1] // width

    def body(h, wg, wu, wd, out, hid):
        t, f = pl.program_id(0), pl.program_id(1)
        hook(t * chunks + f)

        @pl.when(f == 0)
        def _():
            wide = h[...].astype(F32)
            a[...] = (wide * scale_of(wide)).astype(BF16)
            acc[...] = jnp.zeros_like(acc)

        gate = dot(a[...], wg[...], ((1,), (0,)))
        up = dot(a[...], wu[...], ((1,), (0,)))
        hid[...] = (gate * jax.nn.sigmoid(gate) * up).astype(BF16)
        acc[...] += dot(hid[...], wd[...], ((1,), (0,)))

        @pl.when(f == chunks - 1)
        def _():
            out[...] = (h[...].astype(F32) + acc[...].astype(BF16).astype(F32)).astype(BF16)

    whole = pl.BlockSpec((TOKENS, dim), lambda t, f: (t, 0))
    pltpu.emit_pipeline(
        body,
        grid=(tiles, chunks),
        in_specs=[
            whole,
            pl.BlockSpec((dim, width), lambda t, f: (0, f)),
            pl.BlockSpec((dim, width), lambda t, f: (0, f)),
            pl.BlockSpec((width, dim), lambda t, f: (f, 0)),
        ],
        out_specs=[whole, pl.BlockSpec((TOKENS, width), lambda t, f: (t, f))],
    )(h, wg, wu, wd, out, hid)


class Layer:
    def __init__(self, h, dy, wg, wu, wd, dh, a, a_t, h_held, dy_held, acc, dgate, dup, hid, local):
        self.h, self.dy, self.wg, self.wu, self.wd, self.dh = h, dy, wg, wu, wd, dh
        self.a, self.a_t, self.h_held, self.dy_held, self.acc = a, a_t, h_held, dy_held, acc
        self.dgate, self.dup, self.hid, self.local = dgate, dup, hid, local
        self.runs = wg.shape[1] // CHUNK

    def tiles(self):
        return [pl.ds(t * TILE, TILE) for t in range(self.h.shape[0] // TILE)]

    def load(self):
        for n, (src, dst) in enumerate(((self.h, self.h_held), (self.dy, self.dy_held))):
            pltpu.make_async_copy(src, dst, self.local.at[n]).start()

    def wait(self, n):
        src, dst = ((self.h, self.h_held), (self.dy, self.dy_held))[n]
        pltpu.make_async_copy(src, dst, self.local.at[n]).wait()

    def norm(self):
        for rows in self.tiles():
            wide = self.h_held[rows].astype(F32)
            a = (wide * scale_of(wide)).astype(BF16)
            self.a[rows] = a
            self.a_t[:, rows] = a.T
            self.acc[rows] = jnp.zeros((TILE, self.acc.shape[1]), F32)

    def loop(self, stream, hook, dwd):
        def body(wg, wu, wd, *down):
            f = pl.program_id(0)
            hook(f)
            for rows in self.tiles():
                a = self.a[rows]
                gate = dot(a, wg[...], ((1,), (0,)))
                up = dot(a, wu[...], ((1,), (0,)))
                dhid = dot(self.dy_held[rows], wd[...], ((1,), (1,))).astype(BF16).astype(F32)
                s = jax.nn.sigmoid(gate)
                silu = gate * s
                if down:
                    self.hid[rows] = (silu * up).astype(BF16)
                by_gate = (dhid * up * (s * (1 + gate * (1 - s)))).astype(BF16)
                by_up = (dhid * silu).astype(BF16)
                self.dgate[rows] = by_gate
                self.dup[rows] = by_up
                self.acc[rows] += dot(by_gate, wg[...], ((1,), (1,))) + dot(by_up, wu[...], ((1,), (1,)))
            stream.store(0, f, dot(self.a_t[...], self.dgate[...], ((1,), (0,))))
            stream.store(1, f, dot(self.a_t[...], self.dup[...], ((1,), (0,))))
            if down:
                down[0][...] = dot(self.hid[...], self.dy_held[...], ((0,), (0,))).astype(BF16)

        dim = self.wg.shape[0]
        wide = pl.BlockSpec((dim, CHUNK), lambda f: (0, f))
        tall = pl.BlockSpec((CHUNK, dim), lambda f: (f, 0))
        pltpu.emit_pipeline(
            body, grid=(self.runs,), in_specs=[wide, wide, tall], out_specs=[tall] * len(dwd)
        )(self.wg, self.wu, self.wd, *dwd)

    def to_dh(self, rows, t):
        return pltpu.make_async_copy(self.h_held.at[rows], self.dh.at[rows], self.local.at[2 + t])

    def by_h(self):
        for t, rows in enumerate(self.tiles()):
            wide = self.h_held[rows].astype(F32)
            scale = scale_of(wide)
            da = self.acc[rows].astype(BF16).astype(F32)
            along = jnp.mean(da * wide, -1, keepdims=True)
            by_h = (da * scale - wide * (along * scale * scale * scale)).astype(BF16)
            self.h_held[rows] = (self.dy_held[rows].astype(F32) + by_h.astype(F32)).astype(BF16)
            self.to_dh(rows, t).start()

    def close(self):
        for t, rows in enumerate(self.tiles()):
            self.to_dh(rows, t).wait()

    @staticmethod
    def scratch(tokens, dim, keeps_hid):
        return (
            [pltpu.VMEM((tokens, dim), BF16), pltpu.VMEM((dim, tokens), BF16)]
            + [pltpu.VMEM((tokens, dim), BF16)] * 2
            + [pltpu.VMEM((tokens, dim), F32)]
            + [pltpu.VMEM((tokens, CHUNK), BF16)] * 2
            + [pltpu.VMEM((tokens if keeps_hid else 16, CHUNK), BF16)]
            + [pltpu.SemaphoreType.DMA((2 + tokens // TILE,))]
        )


def streamed(stream, others):
    def hook(f):
        def earlier(n, step):
            @pl.when(f >= n)
            def _():
                step(f - n)

        earlier(1, stream.begin)
        earlier(3, stream.send_z)
        earlier(2, stream.send_y)
        earlier(4, stream.finish)
        at_step(others, f)

    return hook


def drained(stream, runs, meanwhile):
    last = runs - 1
    stream.begin(last)
    stream.send_y(last - 1)
    stream.send_z(last - 2)
    stream.send_y(last)
    meanwhile()
    stream.finish(last - 3)
    stream.send_z(last - 1)
    stream.finish(last - 2)
    stream.send_z(last)
    stream.finish(last - 1)
    stream.finish(last)
    stream.close(runs)


def by_down(hid, dy, dwd, hook):
    tokens, dim = dy.shape

    def body(hid, dwd):
        hook(pl.program_id(0))
        dwd[...] = dot(hid[...], dy[...], ((0,), (0,))).astype(BF16)

    pltpu.emit_pipeline(
        body,
        grid=(hid.shape[1] // CHUNK,),
        in_specs=[pl.BlockSpec((tokens, CHUNK), lambda f: (0, f))],
        out_specs=[pl.BlockSpec((CHUNK, dim), lambda f: (f, 0))],
    )(hid, dwd)


def call(body, outs, scratch, collective, *args):
    return pl.pallas_call(
        body,
        out_shape=[jax.ShapeDtypeStruct(shape, BF16) for shape in outs],
        in_specs=[ANY] * len(args),
        out_specs=[ANY] * len(outs),
        scratch_shapes=scratch,
        compiler_params=pltpu.CompilerParams(collective_id=collective, has_side_effects=True, vmem_limit_bytes=VMEM_LIMIT),
    )(*args)


def solution(mesh):
    def step(x, dy, *weights):
        tokens, dim = x.shape[1:]
        ff = weights[0].shape[2]
        x, dy = x[0], dy[0]
        shards = [w.shape[1:] for w in weights]
        wholes = [(16 * r, c) for r, c in shards]
        runs = ff // CHUNK
        n_gather = len(Gather.scratch((8, 128)))
        gather_scratch = [s for shape in shards * 2 for s in Gather.scratch(shape)]
        stream_scratch, layer_scratch = Stream.scratch(shards[0]), Layer.scratch(tokens, dim, True)
        down_scratch = Scatter.scratch(shards[2])
        n_stream, n_layer, n_down = len(stream_scratch), len(layer_scratch), len(down_scratch)

        def gather_forward(*refs):
            h, srcs = refs[0], refs[1:4]
            out, hid, wholes = refs[4], refs[5], refs[6:12]
            a, acc, scratch = refs[12], refs[13], refs[14:]
            place = Place()
            place.greet(True)
            jobs = [
                Gather(place, srcs[i % 3].at[i // 3], wholes[i], *scratch[n_gather * i : n_gather * (i + 1)]) for i in range(6)
            ]
            for job in jobs:
                job.begin()
            for job in jobs:
                job.keep()
            before, events = gather_events(jobs, 3)
            for event in before:
                event()
            early = len(events) * 3 // 5
            steps = (tokens // TOKENS) * (ff // 512)
            forward(h, *wholes[:3], out, hid, a, acc, functools.partial(at_step, spread(events[:early], steps)))
            for event in events[early:]:
                event()

        tile = [pltpu.VMEM((TOKENS, dim), BF16), pltpu.VMEM((TOKENS, dim), F32)]
        h1, hid0, *gathered = call(gather_forward, [(tokens, dim), (tokens, ff), *wholes, *wholes], tile + gather_scratch, 1, x, *weights)
        first, second = gathered[:3], gathered[3:]

        def last_layer(*refs):
            dh, dwd, *sums = refs[5:9]
            layer = Layer(*refs[:5], dh, *refs[9 : 9 + n_layer])
            place = Place()
            place.greet(False)
            stream = Stream(place, sums, *refs[9 + n_layer :])
            layer.load()
            layer.wait(0)
            layer.norm()
            layer.wait(1)
            layer.loop(stream, streamed(stream, []), [dwd])
            drained(stream, runs, layer.by_h)
            layer.close()

        d1, down1, *sums1 = call(
            last_layer, [(tokens, dim), wholes[2], *shards[:2]], layer_scratch + stream_scratch, 2, h1, dy, *second
        )

        def first_layer(*refs):
            hid0, down1 = refs[5:7]
            dh, down0, *sums = refs[7:11]
            sum_down0, sum_down1 = refs[11:13]
            scratch = refs[13:]
            layer = Layer(*refs[:5], dh, *scratch[:n_layer])
            place = Place()
            place.greet(False)
            scratch = scratch[n_layer:]
            stream = Stream(place, sums, *scratch[:n_stream])
            scratch = scratch[n_stream:]
            one = Scatter(place, down1, sum_down1, *scratch[:n_down])
            nought = Scatter(place, down0, sum_down0, *scratch[n_down:])
            layer.load()
            one.begin()
            layer.wait(0)
            layer.norm()
            layer.wait(1)
            sends = {2 + n: [functools.partial(one.send_y, d)] for n, d in enumerate((1, 2, 3, 0))}
            by_down(hid0, layer.dy_held, down0, functools.partial(at_step, [sends.get(n, []) for n in range(runs)]))
            nought.begin()
            others = [
                [functools.partial(one.send_z, 1)],
                [functools.partial(one.send_z, 2), functools.partial(one.send_z, 3), functools.partial(nought.send_y, 1)],
                [functools.partial(nought.send_y, 2)],
                [one.finish, functools.partial(nought.send_z, 1)],
                [functools.partial(nought.send_y, 3), functools.partial(nought.send_z, 2)],
                [functools.partial(nought.send_y, 0)],
                [functools.partial(nought.send_z, 3)],
                [],
                [nought.finish],
            ]
            layer.loop(stream, streamed(stream, others), [])
            drained(stream, runs, layer.by_h)
            layer.close()

        d0, _, *rest = call(
            first_layer,
            [(tokens, dim), wholes[2], *shards[:2], shards[2], shards[2]],
            Layer.scratch(tokens, dim, False) + stream_scratch + down_scratch * 2,
            3,
            x,
            d1,
            *first,
            hid0,
            down1,
        )
        sums0 = rest[:3]
        sums1 = [*sums1, rest[3]]
        return (d0[None], *(jnp.stack(pair) for pair in zip(sums0, sums1)))

    tokens, rows, out = P(("rep", "dp")), P(None, "dp"), P("rep", "dp")
    return jax.shard_map(
        step, mesh=mesh, in_specs=(tokens, tokens, rows, rows, rows), out_specs=(tokens, out, out, out), check_vma=False
    )
```

time: 547 us -> 465 us (0.85)
  Pallas kernels: 538 us -> 450 us
    pallas_call x5 -> x3, Pallas kernels: 538 us -> 450 us  [call(): pl.pallas_call(body, out_shape=[jax.ShapeDtypeStruct(shape, BF16) for sha...]
where the time goes in v2:
time: 465 us; the launch traced here: 459 us
  Pallas kernels  450 us (97%)
    pallas_call x3, Pallas kernels, call(): pl.pallas_call(body, out_shape=[jax.ShapeDtypeStruct(shape, BF16) for sha...  450 us

profile of v2, /device:TPU:0, one launch (start us, length us, event | category | flops | bytes accessed | tf_op | source)
XLA Modules:
  0.0 459.3 jit_solution(10565349293142414410)
XLA Ops:
  0.6 159.4 %shard_map.84 = (bf16[2048,896]{1,0:T(8,128)(2,1)}, bf16[2048,2560]{1,0:T(8,128)(2,1)}, bf16[896,2560]{1,0:T(8,128)(2,1)}, bf16[896,2560]{1,0:T(8,128)(2,1)}, bf...) custom-call(bf16[2048,896]{1,0:T(8,128)(2,1)} %bitcast.9, ...), custom_call_target="tpu_custom_call" | custom-call | tf_op jit(solution)/shard_map/pallas_call | solution.py:538
  160.0 135.9 %shard_map.85 = (bf16[2048,896]{1,0:T(8,128)(2,1)}, bf16[2560,896]{1,0:T(8,128)(2,1)}, bf16[56,2560]{1,0:T(8,128)(2,1)}, bf16[56,2560]{1,0:T(8,128)(2,1)}) custom-call(bf16[2048,896]{1,0:T(8,128)(2,1)} %get-tuple-element.21.refs_0_, bf16[2048,896]{1,0:T(8,128)(2,1)} %bitcast.11, bf16[896,2560]{1,0:T(8,128)(2,1)} %get-tuple-element.22.refs_2_, ...), custom_call_target="tpu_custom_call" | custom-call | tf_op jit(solution)/shard_map/pallas_call | solution.py:538
  296.0 0.0 copy-start
  296.0 154.8 %shard_map.86 = (bf16[2048,896]{1,0:T(8,128)(2,1)}, bf16[2560,896]{1,0:T(8,128)(2,1)}, bf16[56,2560]{1,0:T(8,128)(2,1)}, bf16[56,2560]{1,0:T(8,128)(2,1)}, bf16[...) custom-call(bf16[2048,896]{1,0:T(8,128)(2,1)} %bitcast.10, bf16[2048,896]{1,0:T(8,128)(2,1)} %get-tuple-element.25.refs_1_, ...), custom_call_target="tpu_custom_call" | custom-call | tf_op jit(solution)/shard_map/pallas_call | solution.py:538
  450.8 0.0 copy-done
  450.8 2.2 pad_maximum_fusion
  453.0 1.9 pad_maximum_fusion.2
  455.0 4.2 copy.10
Async XLA Ops:
  296.0 154.8 %copy-start = (bf16[56,2560]{1,0:T(8,128)(2,1)S(1)}, bf16[56,2560]{1,0:T(8,128)(2,1)}, u32[]{:S(2)}) copy-start(bf16[56,2560]{1,0:T(8,128)(2,1)} %get-tuple-element.33) | copy-start | bytes 860164

commit v3 on v2

--- a/solution.py
+++ b/solution.py
@@ -11,7 +11,8 @@
 ANY = pl.BlockSpec(memory_space=pl.ANY)
 VMEM_LIMIT = 66_500_000
 NY, NZ = 2, 4
-TOKENS, TILE, CHUNK, RING = 512, 1024, 256, 4
+PASS = 256
+TOKENS, TILE, CHUNK, RING, AHEAD = 512, 1024, 256, 4, 2
 
 
 def device(y, z, c):
@@ -83,6 +84,8 @@
                 self.copy(self.half(self.src, 0, p.x), self.part(p.me, p.x), d - 1, p.z_mate(d)).start()
         self.copy(self.src, mine, 3, p.y_mate).start()
         self.copy(self.src, mine, 13, p.sibling).start()
+
+    def load(self):
         pltpu.make_async_copy(self.src, self.stage, self.local.at[0]).start()
 
     def keep(self):
@@ -327,6 +330,8 @@
         events = []
         if n < len(jobs):
             events += [functools.partial(jobs[n].from_z, d) for d in (1, 2, 3)]
+        if n + AHEAD < len(jobs):
+            events.append(jobs[n + AHEAD].begin)
         if 0 < n <= len(jobs):
             for d in (0, 1, 2, 3):
                 if d > 1:
@@ -421,12 +426,16 @@
         pltpu.make_async_copy(src, dst, self.local.at[n]).wait()
 
     def norm(self):
-        for rows in self.tiles():
-            wide = self.h_held[rows].astype(F32)
+        def some(t, carry):
+            rows = pl.ds(pl.multiple_of(t * PASS, PASS), PASS)
+            wide = self.h_held[rows, :].astype(F32)
             a = (wide * scale_of(wide)).astype(BF16)
-            self.a[rows] = a
+            self.a[rows, :] = a
             self.a_t[:, rows] = a.T
-            self.acc[rows] = jnp.zeros((TILE, self.acc.shape[1]), F32)
+            self.acc[rows, :] = jnp.zeros((PASS, self.acc.shape[1]), F32)
+            return carry
+
+        lax.fori_loop(0, self.h.shape[0] // PASS, some, 0)
 
     def loop(self, stream, hook, dwd):
         def body(wg, wu, wd, *down):
@@ -458,22 +467,27 @@
             body, grid=(self.runs,), in_specs=[wide, wide, tall], out_specs=[tall] * len(dwd)
         )(self.wg, self.wu, self.wd, *dwd)
 
-    def to_dh(self, rows, t):
-        return pltpu.make_async_copy(self.h_held.at[rows], self.dh.at[rows], self.local.at[2 + t])
+    def to_dh(self, t):
+        rows = pl.ds(pl.multiple_of(t * PASS, PASS), PASS)
+        return pltpu.make_async_copy(self.h_held.at[rows, :], self.dh.at[rows, :], self.local.at[2 + t])
 
     def by_h(self):
-        for t, rows in enumerate(self.tiles()):
-            wide = self.h_held[rows].astype(F32)
+        def some(t, carry):
+            rows = pl.ds(pl.multiple_of(t * PASS, PASS), PASS)
+            wide = self.h_held[rows, :].astype(F32)
             scale = scale_of(wide)
-            da = self.acc[rows].astype(BF16).astype(F32)
+            da = self.acc[rows, :].astype(BF16).astype(F32)
             along = jnp.mean(da * wide, -1, keepdims=True)
             by_h = (da * scale - wide * (along * scale * scale * scale)).astype(BF16)
-            self.h_held[rows] = (self.dy_held[rows].astype(F32) + by_h.astype(F32)).astype(BF16)
-            self.to_dh(rows, t).start()
+            self.h_held[rows, :] = (self.dy_held[rows, :].astype(F32) + by_h.astype(F32)).astype(BF16)
+            self.to_dh(t).start()
+            return carry
+
+        lax.fori_loop(0, self.h.shape[0] // PASS, some, 0)
 
     def close(self):
-        for t, rows in enumerate(self.tiles()):
-            self.to_dh(rows, t).wait()
+        for t in range(self.h.shape[0] // PASS):
+            self.to_dh(t).wait()
 
     @staticmethod
     def scratch(tokens, dim, keeps_hid):
@@ -483,7 +497,7 @@
             + [pltpu.VMEM((tokens, dim), F32)]
             + [pltpu.VMEM((tokens, CHUNK), BF16)] * 2
             + [pltpu.VMEM((tokens if keeps_hid else 16, CHUNK), BF16)]
-            + [pltpu.SemaphoreType.DMA((2 + tokens // TILE,))]
+            + [pltpu.SemaphoreType.DMA((2 + tokens // PASS,))]
         )
 
 
@@ -568,14 +582,16 @@
             jobs = [
                 Gather(place, srcs[i % 3].at[i // 3], wholes[i], *scratch[n_gather * i : n_gather * (i + 1)]) for i in range(6)
             ]
+            for job in jobs[:AHEAD]:
+                job.begin()
             for job in jobs:
-                job.begin()
+                job.load()
             for job in jobs:
                 job.keep()
             before, events = gather_events(jobs, 3)
             for event in before:
                 event()
-            early = len(events) * 3 // 5
+            early = len(events) * 4 // 5
             steps = (tokens // TOKENS) * (ff // 512)
             forward(h, *wholes[:3], out, hid, a, acc, functools.partial(at_step, spread(events[:early], steps)))
             for event in events[early:]:

time: 465 us -> 447 us (0.961)
  Pallas kernels: 450 us -> 437 us
    pallas_call x3, Pallas kernels: 450 us -> 437 us  [call(): pl.pallas_call(body, out_shape=[jax.ShapeDtypeStruct(shape, BF16) for sha...]
where the time goes in v3:
time: 447 us; the launch traced here: 446 us
  Pallas kernels  437 us (98%)
    pallas_call x3, Pallas kernels, call(): pl.pallas_call(body, out_shape=[jax.ShapeDtypeStruct(shape, BF16) for sha...  437 us

profile of v3, /device:TPU:0, one launch (start us, length us, event | category | flops | bytes accessed | tf_op | source)
XLA Modules:
  0.0 445.8 jit_solution(13703948860459359267)
XLA Ops:
  0.6 146.9 %shard_map.84 = (bf16[2048,896]{1,0:T(8,128)(2,1)}, bf16[2048,2560]{1,0:T(8,128)(2,1)}, bf16[896,2560]{1,0:T(8,128)(2,1)}, bf16[896,2560]{1,0:T(8,128)(2,1)}, bf...) custom-call(bf16[2048,896]{1,0:T(8,128)(2,1)} %bitcast.9, ...), custom_call_target="tpu_custom_call" | custom-call | tf_op jit(solution)/shard_map/pallas_call | solution.py:552
  147.6 136.1 %shard_map.85 = (bf16[2048,896]{1,0:T(8,128)(2,1)}, bf16[2560,896]{1,0:T(8,128)(2,1)}, bf16[56,2560]{1,0:T(8,128)(2,1)}, bf16[56,2560]{1,0:T(8,128)(2,1)}) custom-call(bf16[2048,896]{1,0:T(8,128)(2,1)} %get-tuple-element.21.refs_0_, bf16[2048,896]{1,0:T(8,128)(2,1)} %bitcast.11, bf16[896,2560]{1,0:T(8,128)(2,1)} %get-tuple-element.22.refs_2_, ...), custom_call_target="tpu_custom_call" | custom-call | tf_op jit(solution)/shard_map/pallas_call | solution.py:552
  283.7 0.0 copy-start
  283.7 153.8 %shard_map.86 = (bf16[2048,896]{1,0:T(8,128)(2,1)}, bf16[2560,896]{1,0:T(8,128)(2,1)}, bf16[56,2560]{1,0:T(8,128)(2,1)}, bf16[56,2560]{1,0:T(8,128)(2,1)}, bf16[...) custom-call(bf16[2048,896]{1,0:T(8,128)(2,1)} %bitcast.10, bf16[2048,896]{1,0:T(8,128)(2,1)} %get-tuple-element.25.refs_1_, ...), custom_call_target="tpu_custom_call" | custom-call | tf_op jit(solution)/shard_map/pallas_call | solution.py:552
  437.4 0.0 copy-done
  437.5 2.2 pad_maximum_fusion
  439.7 1.9 pad_maximum_fusion.2
  441.6 4.2 copy.10
Async XLA Ops:
  283.7 153.8 %copy-start = (bf16[56,2560]{1,0:T(8,128)(2,1)S(1)}, bf16[56,2560]{1,0:T(8,128)(2,1)}, u32[]{:S(2)}) copy-start(bf16[56,2560]{1,0:T(8,128)(2,1)} %get-tuple-element.33) | copy-start | bytes 860164
